TPU v7x, 256 devices: a whole 4x4x8 slice. The times are simulated.
256 devices in a mesh: dom: 8 (over y, core), mem: 32 (over z, x).
Axes of the slice: x: 4, y: 4, z: 8, core: 2. Of those that a mesh axis runs over, the one named last changes fastest.
Arguments:
- control: bfloat16 [256, 128, 16384], P('mem', None, 'dom'), may hold values from -6 to 6
- corr_offsets: int32 [128, 4], P('dom'), may hold values from -2 to 2, as said below
- corr_blocks: bfloat16 [128, 4, 128, 128], P('dom'), may hold values from -0.25 to 0.25
- interp_index: int32 [128, 4], P('dom'), may hold values from 0 to 15
- interp_blocks: bfloat16 [128, 4, 128, 128], P('dom'), may hold values from -0.25 to 0.25
- perturbations: bfloat16 [256, 128, 16384], P('mem', None, 'dom'), may hold values from -6 to 6
Outputs:
- increment: bfloat16 [128, 16384], P(None, 'dom')
Inputs may be any that keep to these rules, and one draw needn't show every extreme that they name: `corr_offsets`: each row holds 4 distinct offsets, among them 0, -2 and 2; exactly one of -1 and 1 is absent from each row. `interp_index`: an entry names a subgrid block of the tile that owns the column block, counted from that tile's first block.
All inputs are finite; a program needn't handle non-finite values.
Results may differ from a plain program's by a relative error of at most 0.0049.
Values may be sent and summed in bfloat16 or wider, within the bound.
No kernel may reach another device: no remote copies, remote signals or barrier semaphores. Data moves between devices by JAX's collectives and lax.ppermute only.
A program may use at most 128 MiB of HBM per device.

v0:
```python
import jax
import jax.numpy as jnp
from jax import lax
from jax.sharding import PartitionSpec as P

HR = 2


def extended_2(block, sides, width):
    for axis, dim in sides:
        count = lax.axis_size(axis)
        forward = [(i, i + 1) for i in range(count - 1)]
        forward.append((count - 1, 0))
        backward = [(target, source) for source, target in forward]
        low = lax.ppermute(
            lax.slice_in_dim(block, block.shape[dim] - width, None, axis=dim), axis, forward
        )
        high = lax.ppermute(lax.slice_in_dim(block, 0, width, axis=dim), axis, backward)
        block = jnp.concatenate([low, block, high], axis=dim)
    return block


def smooth_blocks(control, corr_offsets, corr_blocks):
    members = control.shape[0]
    levels = control.shape[1]
    blocks = corr_blocks.shape[0]
    breadth = corr_blocks.shape[2]
    extended = extended_2(control, (("dom", 2),), HR * breadth)
    tile_rows = extended.reshape(members * levels, blocks + 2 * HR, breadth)
    source = jnp.arange(blocks, dtype=jnp.int32)[:, None] + HR + corr_offsets
    picked = tile_rows[:, source]
    smoothed = jnp.einsum("rbsj,bsji->rbi", picked, corr_blocks, preferred_element_type=jnp.float32)
    return smoothed.astype(jnp.bfloat16).reshape(members, levels, blocks, breadth)


def member_terms(smoothed, interp_index, interp_blocks, perturbations, level_count):
    members = smoothed.shape[0]
    blocks = smoothed.shape[2]
    breadth = smoothed.shape[3]
    column_blocks = interp_blocks.shape[0]
    feeding = smoothed.reshape(members * level_count, blocks, breadth)[:, interp_index]
    spread = jnp.einsum(
        "rqkj,qkji->rqi", feeding, interp_blocks, preferred_element_type=jnp.float32
    )
    spread = spread.reshape(members, level_count, column_blocks * breadth)
    return jnp.sum(perturbations.astype(jnp.float32) * spread, axis=0)


def per_device(control, corr_offsets, corr_blocks, interp_index, interp_blocks, perturbations):
    smoothed = smooth_blocks(control, corr_offsets, corr_blocks)
    levels = control.shape[1]
    members_all = control.shape[0] * lax.axis_size("mem")
    factor = 1.0 / jnp.sqrt(jnp.float32(members_all - 1))
    local_sum = member_terms(smoothed, interp_index, interp_blocks, perturbations, levels)
    summed = lax.psum(local_sum, "mem")
    return (summed * factor).astype(jnp.bfloat16)


def solution(mesh):
    in_specs = (
        P("mem", None, "dom"),
        P("dom", None),
        P("dom", None, None, None),
        P("dom", None),
        P("dom", None, None, None),
        P("mem", None, "dom"),
    )
    out_specs = P(None, "dom")
    return jax.shard_map(
        per_device, mesh=mesh, in_specs=in_specs, out_specs=out_specs, check_vma=False
    )
```

profile of v0, /device:TPU:24, one launch (start us, length us, event | category | flops | bytes accessed | tf_op | source)
XLA Modules:
  0.0 275.9 jit_solution(11671782922213682755)
XLA Ops:
  6.5 0.0 copy-start
  6.5 0.0 all-reduce.2.cloned.1.call-start
  6.5 2.4 fusion.1
  9.0 0.0 collective-permute-start
  9.0 1.7 collective-permute-start.1
  10.7 0.7 compare_select_fusion
  11.4 0.1 copy.13
  11.5 0.1 reshape.23
  11.6 0.7 compare_select_fusion.1
  12.3 0.1 copy.11
  12.3 0.1 reshape.15
  12.5 5.3 %collective-permute-done = bf16[8,128,256]{2,1,0:T(8,128)(2,1)S(1)} collective-permute-done((bf16[8,128,256]{2,1,0:T(8,128)(2,1)}, bf16[8,128,256]{2,1,0:T(8,128)(2,1)S(1)}, u32[]{:S(2)}, u32[]{:S(2)}) %collective-permute-start) | collective-permute-done | bytes 524320 | tf_op jit(solution)/shard_map/ppermute | solution.py:15
  17.8 0.0 collective-permute-done.1
  17.8 5.0 %pad_maximum_fusion = bf16[8,128,2560]{2,1,0:T(8,128)(2,1)} fusion(bf16[8,128,256]{2,1,0:T(8,128)(2,1)S(1)} %collective-permute-done.1, bf16[8,128,2048]{2,1,0:T(8,128)(2,1)} %param.6, bf16[8,128,256]{2,1,0:T(8,128)(2,1)S(1)} %collective-permute-done), kind=kLoop, calls=%fused_computation.4 | loop fusion | flops 15728640 | bytes 10485760 | tf_op jit(solution)/shard_map/concatenate | solution.py:19
  22.8 10.0 %reshape.35 = bf16[1024,20,128]{2,1,0:T(8,128)(2,1)} reshape(bf16[8,128,2560]{2,1,0:T(8,128)(2,1)} %pad_maximum_fusion) | data formatting | bytes 10485760 | tf_op jit(solution)/shard_map/reshape | solution.py:29
  32.7 6.2 %copy.12 = bf16[1024,20,128]{2,0,1:T(8,128)(2,1)} copy(bf16[1024,20,128]{2,1,0:T(8,128)(2,1)} %reshape.35) | data formatting | bytes 10485760 | tf_op jit(solution)/shard_map/reshape | solution.py:29
  38.9 10.1 %gather_fusion = bf16[64,1024,128]{2,1,0:T(8,128)(2,1)} fusion(bf16[1024,20,128]{2,0,1:T(8,128)(2,1)} %copy.12, s32[1024]{0:T(1024)S(1)} %pad_clamp_fusion.1), kind=kCustom, calls=%fused_computation | custom fusion | bytes 33554688 | tf_op jit(solution)/shard_map/gather | solution.py:31
  49.0 0.0 copy-done
  49.0 12.2 %fusion = bf16[1024,16,128]{2,0,1:T(8,128)(2,1)} fusion(bf16[1024,16,4,128]{3,0,2,1:T(8,128)(2,1)} %bitcast.22, bf16[16,4,128,128]{3,2,1,0:T(8,128)(2,1)S(1)} %copy-done), kind=kOutput, calls=%fused_computation.5 | convolution fusion | flops 2149580800 | bytes 23068672 | tf_op jit(solution)/shard_map/rbsj,bsji->rbi/dot_general | solution.py:32
  61.2 0.0 copy-start.2
  61.2 9.9 %gather_fusion.1 = bf16[64,1024,128]{2,1,0:T(8,128)(2,1)} fusion(bf16[1024,16,128]{2,0,1:T(8,128)(2,1)} %fusion, s32[1024]{0:T(1024)S(1)} %pad_clamp_fusion), kind=kCustom, calls=%fused_computation.1 | custom fusion | bytes 33554688 | tf_op jit(solution)/shard_map/gather | solution.py:41
  71.1 0.0 copy-done.2
  71.1 13.5 %convolution_bitcast_fusion = f32[1024,16,128]{2,0,1:T(8,128)} fusion(bf16[1024,16,4,128]{3,0,2,1:T(8,128)(2,1)} %bitcast.23, bf16[16,4,128,128]{3,2,1,0:T(8,128)(2,1)S(1)} %copy-done.2), kind=kOutput, calls=%fused_computation.6 | convolution fusion | flops 2147483648 | bytes 27262976 | tf_op jit(solution)/shard_map/rqkj,qkji->rqi/dot_general | solution.py:42
  84.6 11.5 %copy.14 = f32[1024,16,128]{2,1,0:T(8,128)} copy(f32[1024,16,128]{2,0,1:T(8,128)} %convolution_bitcast_fusion) | data formatting | bytes 16777216 | tf_op jit(solution)/shard_map/rqkj,qkji->rqi/transpose | solution.py:42
  96.1 0.0 copy-start.1
  96.1 9.4 %reshape.12 = f32[8,128,2048]{2,1,0:T(8,128)} reshape(f32[1024,16,128]{2,1,0:T(8,128)} %copy.14) | data formatting | bytes 16777216 | tf_op jit(solution)/shard_map/reshape | solution.py:45
  105.5 7.0 %multiply_reduce_fusion = f32[128,2048]{1,0:T(8,128)} fusion(f32[8,128,2048]{2,1,0:T(8,128)} %reshape.12, bf16[8,128,2048]{2,1,0:T(8,128)(2,1)} %param.11), kind=kLoop, calls=%fused_computation.3 | loop fusion | flops 6029312 | bytes 13631488 | tf_op jit(solution)/shard_map/reduce_sum | solution.py:46
  112.5 0.0 all-reduce.2.cloned.1.call-update
  112.5 154.4 %all-reduce.2.cloned.1.call-done = f32[128,2048]{1,0:T(8,128)} async-done(((f32[128,2048]{1,0:T(8,128)}), f32[128,2048]{1,0:T(8,128)}) %all-reduce.2.cloned.1.call-update) | async-done | bytes 1048592 | tf_op jit(solution)/shard_map/psum | solution.py:55
  266.9 2.1 multiply_convert_fusion
  269.0 0.0 copy-done.1
  (3 shorter events, 0.0 us)
Async XLA Ops:
  6.5 42.5 %copy-start = (bf16[16,4,128,128]{3,2,1,0:T(8,128)(2,1)S(1)}, bf16[16,4,128,128]{3,2,1,0:T(8,128)(2,1)}, u32[]{:S(2)}) copy-start(bf16[16,4,128,128]{3,2,1,0:T(8,128)(2,1)} %param.8) | copy-start | bytes 6291460
  6.5 260.4 %all-reduce.2.cloned.1.call-start = ((), (), s32[]{:S(2)}) async-start(), calls=%async_computation | async-start | bytes 2097152 | tf_op jit(solution)/shard_map/psum | solution.py:55
  9.0 8.8 %collective-permute-start = (bf16[8,128,256]{2,1,0:T(8,128)(2,1)}, bf16[8,128,256]{2,1,0:T(8,128)(2,1)S(1)}, u32[]{:S(2)}, u32[]{:S(2)}) collective-permute-start(bf16[8,128,256]{2,1,0:T(8,128)(2,1)} %get-tuple-element.5), channel_id=1, source_target_pairs={{0,32},{32,64},{64,96},{96,128},{128,160},{160,192},{192,224},{224... | collective-permute-start | bytes 1572872 | tf_op jit(solution)/shard_map/ppermute | solution.py:15
  9.0 8.8 %collective-permute-start.1 = (bf16[8,128,256]{2,1,0:T(8,128)(2,1)}, bf16[8,128,256]{2,1,0:T(8,128)(2,1)S(1)}, u32[]{:S(2)}, u32[]{:S(2)}) collective-permute-start(bf16[8,128,256]{2,1,0:T(8,128)(2,1)} %get-tuple-element.6), channel_id=1, source_target_pairs={{32,0},{64,32},{96,64},{128,96},{160,128},{192,160},{224,192},{0,2... | collective-permute-start | bytes 1572872 | tf_op jit(solution)/shard_map/ppermute | solution.py:18
  61.2 9.9 %copy-start.2 = (bf16[16,4,128,128]{3,2,1,0:T(8,128)(2,1)S(1)}, bf16[16,4,128,128]{3,2,1,0:T(8,128)(2,1)}, u32[]{:S(2)}) copy-start(bf16[16,4,128,128]{3,2,1,0:T(8,128)(2,1)} %param.10) | copy-start | bytes 6291460
  96.1 172.9 %copy-start.1 = (bf16[16,4,128,128]{3,2,1,0:T(8,128)(2,1)S(1)}, bf16[16,4,128,128]{3,2,1,0:T(8,128)(2,1)}, u32[]{:S(2)}) copy-start(bf16[16,4,128,128]{3,2,1,0:T(8,128)(2,1)} %param.8) | copy-start | bytes 6291460
Sparse Core Ops, SparseCore 0:
  112.6 154.2 all-reduce.1
where the time goes:
time: 277 us; the launch traced here: 276 us
  waiting for transfers between devices  160 us (58%)
  local copies, waits for them, and re-layouts  59.7 us (22%)
  matrix products  25.7 us (9%)
  other arithmetic  15.5 us (6%)
  between operations  13.4 us (5%)
    psum x1, waiting for transfers between devices, per_device(): summed = lax.psum(local_sum, 'mem')  154 us
    reshape x2, local copies, waits for them, and re-layouts, smooth_blocks(): tile_rows = extended.reshape(members * levels, blocks + 2 * HR, breadth)  16.1 us
    dot_general x1, matrix products, member_terms(): jnp.einsum('rqkj,qkji->rqi', feeding, interp_blocks, preferred_element_ty...  13.5 us
    dot_general x1, matrix products, smooth_blocks(): jnp.einsum('rbsj,bsji->rbi', picked, corr_blocks, preferred_element_type=...  12.2 us
    transpose x1, local copies, waits for them, and re-layouts, member_terms(): jnp.einsum('rqkj,qkji->rqi', feeding, interp_blocks, preferred_element_ty...  11.5 us
    gather x1, local copies, waits for them, and re-layouts, smooth_blocks(): picked = tile_rows[:, source]  10.1 us
    gather x1, local copies, waits for them, and re-layouts, member_terms(): smoothed.reshape(members * level_count, blocks, breadth)[:, interp_index]  9.89 us
    reshape x1, local copies, waits for them, and re-layouts, member_terms(): spread = spread.reshape(members, level_count, column_blocks * breadth)  9.4 us
  transfers between devices with their start and end apart: 3, of which 2 were waited for; matrix products, arithmetic and copies ran while one was open for 1% of the time, Pallas kernels for 0%

commit v1 on v0

v1 whole, which is shorter than its diff:
```python
import jax
import jax.numpy as jnp
from jax import lax
from jax.experimental import pallas as pl
from jax.experimental.pallas import tpu as pltpu
from jax.sharding import PartitionSpec as P

HR = 2
ANY = pl.BlockSpec(memory_space=pl.ANY)
SMEM = pl.BlockSpec(memory_space=pltpu.SMEM)
VMEM = pl.BlockSpec(memory_space=pltpu.VMEM)


def ring_halos(control, width):
    count = lax.axis_size("dom")
    forward = [(i, (i + 1) % count) for i in range(count)]
    backward = [(target, source) for source, target in forward]
    low = lax.ppermute(control[:, -width:], "dom", forward)
    high = lax.ppermute(control[:, :width], "dom", backward)
    return low, high


def smooth_inner(control, corr_offsets, corr_blocks):
    rows, width = control.shape
    blocks, stored, breadth = corr_blocks.shape[:3]
    inner = blocks - 2 * HR
    depth = stored * breadth
    pair = 2 * breadth

    def kernel(offsets, control_hbm, corr_hbm, out_hbm, tile, corr, out, tile_sem, corr_sem, out_sem):
        def tile_copy(c):
            return pltpu.make_async_copy(
                control_hbm.at[:, pl.ds(c * pair, pair)],
                tile.at[:, pl.ds(c * pair, pair)],
                tile_sem.at[c],
            )

        def corr_copy(c):
            return pltpu.make_async_copy(
                corr_hbm.at[pl.ds(HR + 2 * c, 2)], corr.at[pl.ds(2 * c, 2)], corr_sem.at[c]
            )

        for c in range(4):
            tile_copy(c).start()
        for c in range(2):
            corr_copy(c).start()
        tile_copy(0).wait()
        tile_copy(1).wait()
        for c in range(inner // 2):
            tile_copy(c + 2).wait()
            corr_copy(c).wait()
            if c + 4 < blocks // 2:
                tile_copy(c + 4).start()
            if c + 2 < inner // 2:
                corr_copy(c + 2).start()
            for i in (2 * c, 2 * c + 1):
                sources = [
                    tile[:, pl.ds(pl.multiple_of((HR + i + offsets[s, HR + i]) * breadth, breadth), breadth)]
                    for s in range(stored)
                ]
                result = jnp.dot(
                    jnp.concatenate(sources, axis=1),
                    corr[i].reshape(depth, breadth),
                    preferred_element_type=jnp.float32,
                )
                out[i] = result.astype(jnp.bfloat16)
            pltpu.make_async_copy(
                out.at[pl.ds(2 * c, 2)], out_hbm.at[pl.ds(2 * c, 2)], out_sem.at[c]
            ).start()
        for c in range(inner // 2):
            pltpu.make_async_copy(
                out.at[pl.ds(2 * c, 2)], out_hbm.at[pl.ds(2 * c, 2)], out_sem.at[c]
            ).wait()

    return pl.pallas_call(
        kernel,
        out_shape=jax.ShapeDtypeStruct((inner, rows, breadth), jnp.bfloat16),
        in_specs=[SMEM, ANY, ANY],
        out_specs=ANY,
        scratch_shapes=[
            pltpu.VMEM((rows, width), jnp.bfloat16),
            pltpu.VMEM((inner, stored, breadth, breadth), jnp.bfloat16),
            pltpu.VMEM((inner, rows, breadth), jnp.bfloat16),
            pltpu.SemaphoreType.DMA((blocks // 2,)),
            pltpu.SemaphoreType.DMA((inner // 2,)),
            pltpu.SemaphoreType.DMA((inner // 2,)),
        ],
        compiler_params=pltpu.CompilerParams(vmem_limit_bytes=60 * 1024 * 1024),
        cost_estimate=pl.CostEstimate(
            flops=2 * rows * depth * breadth * inner,
            bytes_accessed=2 * rows * (width + inner * breadth),
            transcendentals=0,
        ),
        name="smooth_inner",
    )(corr_offsets.T, control, corr_blocks)


def member_sums(
    control, low, high, inner_smoothed, corr_offsets, corr_blocks, interp_index, interp_blocks,
    perturbations, members, xs,
):
    rows, width = control.shape
    blocks, stored, breadth = corr_blocks.shape[:3]
    column_blocks, feeding = interp_blocks.shape[:2]
    levels = rows // members
    part = levels // xs
    halo = HR * breadth
    inner = blocks - 2 * HR
    pair = 2 * breadth

    def kernel(
        offsets, index, control_hbm, low_hbm, high_hbm, inner_hbm, corr_hbm, interp_hbm, pert_hbm,
        out, left, right, corr, smoothed, interp, pert, edge_sem, inner_sem, interp_sem, pert_sem,
    ):
        edge = [
            pltpu.make_async_copy(low_hbm, left.at[:, pl.ds(0, halo)], edge_sem.at[0]),
            pltpu.make_async_copy(
                control_hbm.at[:, pl.ds(0, 2 * halo)], left.at[:, pl.ds(halo, 2 * halo)], edge_sem.at[1]
            ),
            pltpu.make_async_copy(corr_hbm.at[pl.ds(0, HR)], corr.at[pl.ds(0, HR)], edge_sem.at[2]),
            pltpu.make_async_copy(
                control_hbm.at[:, pl.ds(width - 2 * halo, 2 * halo)],
                right.at[:, pl.ds(0, 2 * halo)],
                edge_sem.at[3],
            ),
            pltpu.make_async_copy(high_hbm, right.at[:, pl.ds(2 * halo, halo)], edge_sem.at[4]),
            pltpu.make_async_copy(
                corr_hbm.at[pl.ds(blocks - HR, HR)], corr.at[pl.ds(HR, HR)], edge_sem.at[5]
            ),
        ]
        inner_copy = pltpu.make_async_copy(inner_hbm, smoothed.at[pl.ds(HR, inner)], inner_sem)

        def column_copies(c):
            return (
                pltpu.make_async_copy(
                    interp_hbm.at[pl.ds(2 * c, 2)], interp.at[pl.ds(2 * c, 2)], interp_sem.at[c]
                ),
                pltpu.make_async_copy(
                    pert_hbm.at[:, pl.ds(c * pair, pair)],
                    pert.at[:, pl.ds(c * pair, pair)],
                    pert_sem.at[c],
                ),
            )

        for copy in edge:
            copy.start()
        for side in range(2):
            for copy in edge[3 * side : 3 * side + 3]:
                copy.wait()
            if side == 0:
                inner_copy.start()
            for copy in column_copies(side):
                copy.start()
            span = right if side else left
            for i in range(HR):
                b = blocks - HR + i if side else i
                first = blocks - 2 * HR if side else -HR
                sources = [
                    span[:, pl.ds(pl.multiple_of((b - first + offsets[s, b]) * breadth, breadth), breadth)]
                    for s in range(stored)
                ]
                result = jnp.dot(
                    jnp.concatenate(sources, axis=1),
                    corr[side * HR + i].reshape(stored * breadth, breadth),
                    preferred_element_type=jnp.float32,
                )
                smoothed[b] = result.astype(jnp.bfloat16)
        inner_copy.wait()
        for c in range(column_blocks // 2):
            for copy in column_copies(c):
                copy.wait()
            if c + 2 < column_blocks // 2:
                for copy in column_copies(c + 2):
                    copy.start()
            for i in range(2):
                q = 2 * c + i
                lhs = jnp.concatenate([smoothed[index[k, q]] for k in range(feeding)], axis=1)
                spread = jnp.dot(
                    lhs, interp[q].reshape(feeding * breadth, breadth), preferred_element_type=jnp.float32
                )
                term = pert[:, pl.ds(q * breadth, breadth)].astype(jnp.float32) * spread
                total = jnp.sum(term.reshape(members, levels, breadth), axis=0).astype(jnp.bfloat16)
                for x in range(xs):
                    out[c * xs + x, :, i * breadth : (i + 1) * breadth] = total[x * part : (x + 1) * part]

    return pl.pallas_call(
        kernel,
        out_shape=jax.ShapeDtypeStruct((column_blocks // 2 * xs, part, pair), jnp.bfloat16),
        in_specs=[SMEM, SMEM] + [ANY] * 7,
        out_specs=VMEM,
        scratch_shapes=[
            pltpu.VMEM((rows, 3 * halo), jnp.bfloat16),
            pltpu.VMEM((rows, 3 * halo), jnp.bfloat16),
            pltpu.VMEM((2 * HR, stored, breadth, breadth), jnp.bfloat16),
            pltpu.VMEM((blocks, rows, breadth), jnp.bfloat16),
            pltpu.VMEM((column_blocks, feeding, breadth, breadth), jnp.bfloat16),
            pltpu.VMEM((rows, width), jnp.bfloat16),
            pltpu.SemaphoreType.DMA((6,)),
            pltpu.SemaphoreType.DMA,
            pltpu.SemaphoreType.DMA((column_blocks // 2,)),
            pltpu.SemaphoreType.DMA((column_blocks // 2,)),
        ],
        compiler_params=pltpu.CompilerParams(vmem_limit_bytes=60 * 1024 * 1024),
        cost_estimate=pl.CostEstimate(
            flops=2 * rows * feeding * breadth * breadth * (column_blocks + 2 * HR),
            bytes_accessed=6 * rows * width,
            transcendentals=0,
        ),
        name="member_sums",
    )(
        corr_offsets.T, interp_index.T, control, low, high, inner_smoothed, corr_blocks,
        interp_blocks, perturbations,
    )


def sum_received(parts, factor, repeats):
    def kernel(parts_ref, out_ref):
        total = jnp.sum(parts_ref[...].astype(jnp.float32), axis=0) * factor
        out_ref[...] = jnp.broadcast_to(total.astype(jnp.bfloat16)[None], out_ref.shape)

    return pl.pallas_call(
        kernel,
        out_shape=jax.ShapeDtypeStruct((repeats,) + parts.shape[1:], jnp.bfloat16),
        in_specs=[VMEM],
        out_specs=VMEM,
        compiler_params=pltpu.CompilerParams(vmem_limit_bytes=8 * 1024 * 1024),
        name="sum_received",
    )(parts)


def assemble(position, pieces):
    xs = len(pieces)
    zs, part, pair = pieces[0].shape

    def kernel(position_ref, *refs):
        out = refs[-1]
        for k in range(xs):
            x = lax.rem(position_ref[0] + xs - k, xs)
            rows = pl.ds(pl.multiple_of(x * part, part), part)
            for z in range(zs):
                out[rows, z * pair : (z + 1) * pair] = refs[k][z]

    return pl.pallas_call(
        kernel,
        out_shape=jax.ShapeDtypeStruct((xs * part, zs * pair), jnp.bfloat16),
        in_specs=[SMEM] + [VMEM] * xs,
        out_specs=VMEM,
        compiler_params=pltpu.CompilerParams(vmem_limit_bytes=8 * 1024 * 1024),
        name="assemble",
    )(position, *pieces)


def per_device(control, corr_offsets, corr_blocks, interp_index, interp_blocks, perturbations):
    members, levels, width = control.shape
    breadth = corr_blocks.shape[2]
    xs = lax.axis_size("x")
    zs = lax.axis_size("z")
    members_all = members * zs * xs
    factor = float(1.0 / (members_all - 1) ** 0.5)
    rows = control.reshape(members * levels, width)
    low, high = ring_halos(rows, HR * breadth)
    inner = smooth_inner(rows, corr_offsets, corr_blocks)
    sums = member_sums(
        rows, low, high, inner, corr_offsets, corr_blocks, interp_index, interp_blocks,
        perturbations.reshape(members * levels, width), members, xs,
    )
    parts = lax.all_to_all(sums, ("z", "x"), 0, 0)
    share = sum_received(parts, factor, zs)
    column = lax.all_to_all(share, "z", 0, 0)
    pieces = [column]
    for k in range(1, xs):
        pieces.append(lax.ppermute(column, "x", [(i, (i + k) % xs) for i in range(xs)]))
    position = lax.axis_index("x").astype(jnp.int32).reshape(1)
    return assemble(position, pieces)


def solution(mesh):
    zs = 8
    xs = mesh.shape["mem"] // zs
    inner_mesh = jax.sharding.Mesh(
        mesh.devices.reshape(mesh.shape["dom"], zs, xs), ("dom", "z", "x")
    )
    mem = ("z", "x")
    in_specs = (
        P(mem, None, "dom"),
        P("dom", None),
        P("dom", None, None, None),
        P("dom", None),
        P("dom", None, None, None),
        P(mem, None, "dom"),
    )
    out_specs = P(None, "dom")
    return jax.shard_map(
        per_device, mesh=inner_mesh, in_specs=in_specs, out_specs=out_specs, check_vma=False
    )
```

time: 277 us -> 75.8 us (0.27)
  waiting for transfers between devices: 160 us -> 7.32 us
  local copies, waits for them, and re-layouts: 59.7 us -> 2.07 us
  blocking collectives: 0 us -> 42.6 us
  matrix products: 25.7 us -> 0 us
  Pallas kernels: 0 us -> 19.5 us
  other arithmetic: 15.5 us -> 0 us
  between operations: 13.4 us -> 0.04 us
    psum x1 -> x0, waiting for transfers between devices: 154 us -> none  [per_device(): summed = lax.psum(local_sum, 'mem')]
    all_to_all x0 -> x2, blocking collectives: none -> 42.6 us  [the longest x1 29.5 us: per_device(): parts = lax.all_to_all(sums, ('z', 'x'), 0, 0)]
    dot_general x2 -> x0, matrix products: 25.7 us -> none  [the longest x1 13.5 us: member_terms(): jnp.einsum('rqkj,qkji->rqi', feeding, interp_blocks, preferred_element_ty...]
    reshape x3 -> x0, local copies, waits for them, and re-layouts: 25.5 us -> none  [the longest x2 16.1 us: smooth_blocks(): tile_rows = extended.reshape(members * levels, blocks + 2 * HR, breadth)]
    gather x2 -> x0, local copies, waits for them, and re-layouts: 20 us -> none  [the longest x1 10.1 us: smooth_blocks(): picked = tile_rows[:, source]]
    pallas_call x0 -> x4, Pallas kernels: none -> 19.5 us  [the longest x1 11.1 us: member_sums(): pl.pallas_call(kernel, out_shape=jax.ShapeDtypeStruct((column_blocks // 2...]
    transpose x1 -> x0, local copies, waits for them, and re-layouts: 11.5 us -> none  [member_terms(): jnp.einsum('rqkj,qkji->rqi', feeding, interp_blocks, preferred_element_ty...]
    reduce_sum x1 -> x0, other arithmetic: 7 us -> none  [member_terms(): return jnp.sum(perturbations.astype(jnp.float32) * spread, axis=0)]
  transfers between devices with their start and end apart: 3 -> 5, of which waited for: 2 -> 4; matrix products, arithmetic and copies ran while one was open for 1% -> 0% of each run, Pallas kernels for 0% -> 10%
where the time goes in v1:
time: 75.8 us; the launch traced here: 75.5 us
  blocking collectives  42.6 us (56%)
  Pallas kernels  19.5 us (26%)
  waiting for transfers between devices  7.32 us (10%)
  starting transfers between devices  3.97 us (5%)
  local copies, waits for them, and re-layouts  2.07 us (3%)
    all_to_all x1, blocking collectives, per_device(): parts = lax.all_to_all(sums, ('z', 'x'), 0, 0)  29.5 us
    all_to_all x1, blocking collectives, per_device(): column = lax.all_to_all(share, 'z', 0, 0)  13 us
    pallas_call x1, Pallas kernels, member_sums(): pl.pallas_call(kernel, out_shape=jax.ShapeDtypeStruct((column_blocks // 2...  11.1 us
    pallas_call x1, Pallas kernels, smooth_inner(): pl.pallas_call(kernel, out_shape=jax.ShapeDtypeStruct((inner, rows, bread...  7.47 us
    ppermute x3, waiting for transfers between devices, per_device(): lax.ppermute(column, 'x', [(i, (i + k) % xs) for i in range(xs)])  6.53 us
    ppermute x3, starting transfers between devices, per_device(): lax.ppermute(column, 'x', [(i, (i + k) % xs) for i in range(xs)])  3.44 us
  transfers between devices with their start and end apart: 5, of which 4 were waited for; matrix products, arithmetic and copies ran while one was open for 0% of the time, Pallas kernels for 10%

profile of v1, /device:TPU:24, one launch (start us, length us, event | category | flops | bytes accessed | tf_op | source)
XLA Modules:
  0.0 75.5 jit_solution(2933893586881249251)
XLA Ops:
  0.0 1.3 %fusion = (bf16[1024,256]{1,0:T(8,128)(2,1)S(1)}, bf16[1024,256]{1,0:T(8,128)(2,1)S(1)}) fusion(bf16[1024,2048]{1,0:T(8,128)(2,1)} %bitcast.5), kind=kLoop, calls=%fused_computation | loop fusion | bytes 2097152 | tf_op jit(solution)/shard_map/slice | solution.py:19
  1.3 0.2 collective-permute-start.1
  1.5 0.3 collective-permute-start
  1.8 7.5 %smooth_inner.1.inner_hbm = bf16[12,1024,128]{2,1,0:T(8,128)(2,1)} custom-call(s32[4,16]{1,0:T(4,128)} %bitcast.9, bf16[1024,2048]{1,0:T(8,128)(2,1)} %bitcast.6, bf16[16,4,128,128]{3,2,1,0:T(8,128)(2,1)} %corr_hbm.3), custom_call_target="tpu_custom_call" | custom-call | flops 1610612736 | bytes 7340032 | tf_op jit(solution)/shard_map/smooth_inner/pallas_call | solution.py:75
  9.3 0.0 collective-permute-done.1.high_hbm
  9.3 0.0 copy-start
  9.3 0.8 %collective-permute-done.low_hbm = bf16[1024,256]{1,0:T(8,128)(2,1)S(1)} collective-permute-done((bf16[1024,256]{1,0:T(8,128)(2,1)S(1)}, bf16[1024,256]{1,0:T(8,128)(2,1)S(1)}, u32[]{:S(2)}, u32[]{:S(2)}) %collective-permute-start) | collective-permute-done | bytes 524320 | tf_op jit(solution)/shard_map/ppermute | solution.py:18
  10.1 0.0 copy-start.1
  10.1 0.0 copy-done
  10.1 0.8 %copy-done.1 = bf16[1024,256]{1,0:T(8,128)(2,1)} copy-done((bf16[1024,256]{1,0:T(8,128)(2,1)}, bf16[1024,256]{1,0:T(8,128)(2,1)S(1)}, u32[]{:S(2)}) %copy-start.1) | copy-done | bytes 524312
  10.9 11.1 %member_sums.1 = bf16[32,32,256]{2,1,0:T(8,128)(2,1)} custom-call(s32[4,16]{1,0:T(4,128)} %bitcast.10, s32[4,16]{1,0:T(4,128)} %bitcast.11, bf16[1024,2048]{1,0:T(8,128)(2,1)} %bitcast.7, bf16[1024,256]{1,0:T(8,128)(2,1)} %copy-done.1, bf16[1024,256]{1,0:T(8,128)(2,1)} %copy-done, bf16[12,1024,128]{2,1,0:T(8,128)(2,1)} %smooth_inner.1.inner_hbm, ...), custom_call_target="tpu_custom_call" | custom-call | flops 2684354560 | bytes 12582912 | tf_op jit(solution)/shard_map/member_sums/pallas_call | solution.py:186
  22.0 29.5 %all_to_all.10.parts_ref = bf16[32,32,256]{2,1,0:T(8,128)(2,1)S(1)} all-to-all(bf16[32,32,256]{2,1,0:T(8,128)(2,1)} %member_sums.1), channel_id=1, replica_groups=mesh['dom'=8,'z'=8,'x'=4] {'z','x'}, dimensions={0} | all-to-all | bytes 1048576 | tf_op jit(solution)/shard_map/all_to_all | solution.py:267
  51.5 0.1 sum_received.1
  51.6 13.0 %all_to_all.11.refs_0_ = bf16[8,32,256]{2,1,0:T(8,128)(2,1)S(1)} all-to-all(bf16[8,32,256]{2,1,0:T(8,128)(2,1)S(1)} %sum_received.1), channel_id=1, replica_groups=mesh['dom'=8,'z'=8,'x'=4] {'z'}, dimensions={0} | all-to-all | bytes 262144 | tf_op jit(solution)/shard_map/all_to_all | solution.py:269
  64.7 1.7 %collective-permute-start.4 = (bf16[8,32,256]{2,1,0:T(8,128)(2,1)S(1)}, bf16[8,32,256]{2,1,0:T(8,128)(2,1)S(1)}, u32[]{:S(2)}, u32[]{:S(2)}) collective-permute-start(bf16[8,32,256]{2,1,0:T(8,128)(2,1)S(1)} %all_to_all.11.refs_0_), channel_id=1, source_target_pairs={{0,3},{1,0},{2,1},{3,2},{4,7},{5,4},{6,5},{7,6},{8,11},{9,8},{10,9... | collective-permute-start | bytes 393224 | tf_op jit(solution)/shard_map/ppermute | solution.py:272
  66.4 0.9 %collective-permute-start.3 = (bf16[8,32,256]{2,1,0:T(8,128)(2,1)S(1)}, bf16[8,32,256]{2,1,0:T(8,128)(2,1)S(1)}, u32[]{:S(2)}, u32[]{:S(2)}) collective-permute-start(bf16[8,32,256]{2,1,0:T(8,128)(2,1)S(1)} %all_to_all.11.refs_0_), channel_id=1, source_target_pairs={{0,2},{1,3},{2,0},{3,1},{4,6},{5,7},{6,4},{7,5},{8,10},{9,11},{10,... | collective-permute-start | bytes 393224 | tf_op jit(solution)/shard_map/ppermute | solution.py:272
  67.2 0.9 %collective-permute-start.2 = (bf16[8,32,256]{2,1,0:T(8,128)(2,1)S(1)}, bf16[8,32,256]{2,1,0:T(8,128)(2,1)S(1)}, u32[]{:S(2)}, u32[]{:S(2)}) collective-permute-start(bf16[8,32,256]{2,1,0:T(8,128)(2,1)S(1)} %all_to_all.11.refs_0_), channel_id=1, source_target_pairs={{0,1},{1,2},{2,3},{3,0},{4,5},{5,6},{6,7},{7,4},{8,9},{9,10},{10,1... | collective-permute-start | bytes 393224 | tf_op jit(solution)/shard_map/ppermute | solution.py:272
  68.1 2.4 %collective-permute-done.4.refs_3_ = bf16[8,32,256]{2,1,0:T(8,128)(2,1)S(1)} collective-permute-done((bf16[8,32,256]{2,1,0:T(8,128)(2,1)S(1)}, bf16[8,32,256]{2,1,0:T(8,128)(2,1)S(1)}, u32[]{:S(2)}, u32[]{:S(2)}) %collective-permute-start.4) | collective-permute-done | bytes 131104 | tf_op jit(solution)/shard_map/ppermute | solution.py:272
  70.5 2.7 %collective-permute-done.3.refs_2_ = bf16[8,32,256]{2,1,0:T(8,128)(2,1)S(1)} collective-permute-done((bf16[8,32,256]{2,1,0:T(8,128)(2,1)S(1)}, bf16[8,32,256]{2,1,0:T(8,128)(2,1)S(1)}, u32[]{:S(2)}, u32[]{:S(2)}) %collective-permute-start.3) | collective-permute-done | bytes 131104 | tf_op jit(solution)/shard_map/ppermute | solution.py:272
  73.2 1.4 %collective-permute-done.2.refs_1_ = bf16[8,32,256]{2,1,0:T(8,128)(2,1)S(1)} collective-permute-done((bf16[8,32,256]{2,1,0:T(8,128)(2,1)S(1)}, bf16[8,32,256]{2,1,0:T(8,128)(2,1)S(1)}, u32[]{:S(2)}, u32[]{:S(2)}) %collective-permute-start.2) | collective-permute-done | bytes 131104 | tf_op jit(solution)/shard_map/ppermute | solution.py:272
  74.6 0.8 %assemble.1 = bf16[128,2048]{1,0:T(8,128)(2,1)} custom-call(s32[1]{0:T(128)} %bitcast.position_ref, bf16[8,32,256]{2,1,0:T(8,128)(2,1)S(1)} %all_to_all.11.refs_0_, bf16[8,32,256]{2,1,0:T(8,128)(2,1)S(1)} %collective-permute-done.2.refs_1_, bf16[8,32,256]{2,1,0:T(8,128)(2,1)S(1)} %collective-permute-done.3.refs_2_, ...), custom_call_target="tpu_custom_call" | custom-call | tf_op jit(solution)/shard_map/assemble/pallas_call | solution.py:243
Async XLA Ops:
  1.3 8.0 %collective-permute-start.1 = (bf16[1024,256]{1,0:T(8,128)(2,1)S(1)}, bf16[1024,256]{1,0:T(8,128)(2,1)S(1)}, u32[]{:S(2)}, u32[]{:S(2)}) collective-permute-start(bf16[1024,256]{1,0:T(8,128)(2,1)S(1)} %get-tuple-element.5), channel_id=1, source_target_pairs={{32,0},{64,32},{96,64},{128,96},{160,128},{192,160},{224,192},{0,2... | collective-permute-start | bytes 1572872 | tf_op jit(solution)/shard_map/ppermute | solution.py:19
  1.5 8.6 %collective-permute-start = (bf16[1024,256]{1,0:T(8,128)(2,1)S(1)}, bf16[1024,256]{1,0:T(8,128)(2,1)S(1)}, u32[]{:S(2)}, u32[]{:S(2)}) collective-permute-start(bf16[1024,256]{1,0:T(8,128)(2,1)S(1)} %get-tuple-element.6), channel_id=1, source_target_pairs={{0,32},{32,64},{64,96},{96,128},{128,160},{160,192},{192,224},{224... | collective-permute-start | bytes 1572872 | tf_op jit(solution)/shard_map/ppermute | solution.py:18
  9.3 0.8 %copy-start = (bf16[1024,256]{1,0:T(8,128)(2,1)}, bf16[1024,256]{1,0:T(8,128)(2,1)S(1)}, u32[]{:S(2)}) copy-start(bf16[1024,256]{1,0:T(8,128)(2,1)S(1)} %collective-permute-done.1.high_hbm) | copy-start | bytes 1572868
  10.1 0.8 %copy-start.1 = (bf16[1024,256]{1,0:T(8,128)(2,1)}, bf16[1024,256]{1,0:T(8,128)(2,1)S(1)}, u32[]{:S(2)}) copy-start(bf16[1024,256]{1,0:T(8,128)(2,1)S(1)} %collective-permute-done.low_hbm) | copy-start | bytes 1572868
  64.7 5.8 %collective-permute-start.4 = (bf16[8,32,256]{2,1,0:T(8,128)(2,1)S(1)}, bf16[8,32,256]{2,1,0:T(8,128)(2,1)S(1)}, u32[]{:S(2)}, u32[]{:S(2)}) collective-permute-start(bf16[8,32,256]{2,1,0:T(8,128)(2,1)S(1)} %all_to_all.11.refs_0_), channel_id=1, source_target_pairs={{0,3},{1,0},{2,1},{3,2},{4,7},{5,4},{6,5},{7,6},{8,11},{9,8},{10,9... | collective-permute-start | bytes 393224 | tf_op jit(solution)/shard_map/ppermute | solution.py:272
  66.4 6.8 %collective-permute-start.3 = (bf16[8,32,256]{2,1,0:T(8,128)(2,1)S(1)}, bf16[8,32,256]{2,1,0:T(8,128)(2,1)S(1)}, u32[]{:S(2)}, u32[]{:S(2)}) collective-permute-start(bf16[8,32,256]{2,1,0:T(8,128)(2,1)S(1)} %all_to_all.11.refs_0_), channel_id=1, source_target_pairs={{0,2},{1,3},{2,0},{3,1},{4,6},{5,7},{6,4},{7,5},{8,10},{9,11},{10,... | collective-permute-start | bytes 393224 | tf_op jit(solution)/shard_map/ppermute | solution.py:272
  67.2 7.4 %collective-permute-start.2 = (bf16[8,32,256]{2,1,0:T(8,128)(2,1)S(1)}, bf16[8,32,256]{2,1,0:T(8,128)(2,1)S(1)}, u32[]{:S(2)}, u32[]{:S(2)}) collective-permute-start(bf16[8,32,256]{2,1,0:T(8,128)(2,1)S(1)} %all_to_all.11.refs_0_), channel_id=1, source_target_pairs={{0,1},{1,2},{2,3},{3,0},{4,5},{5,6},{6,7},{7,4},{8,9},{9,10},{10,1... | collective-permute-start | bytes 393224 | tf_op jit(solution)/shard_map/ppermute | solution.py:272

commit v2 on v0

v2 whole, which is shorter than its diff:
```python
import jax
import jax.numpy as jnp
from jax import lax
from jax.experimental import pallas as pl
from jax.experimental.pallas import tpu as pltpu
from jax.sharding import PartitionSpec as P

HR = 2
GROUPS = ((2,), (1,), (3,), (0,))
STAGES = (2, 6)
K1_LIMIT = 24
K2_LIMIT = 24
HBM = pl.BlockSpec(memory_space=pltpu.HBM)
VMEM = pl.BlockSpec(memory_space=pltpu.VMEM)


def in_hbm(array):
    return pltpu.with_memory_space_constraint(array, pltpu.HBM)


def tile_halos(rows, width):
    span = rows.shape[1] - width

    def kernel(rows_hbm, first, second, sem):
        odd = lax.rem(lax.axis_index("dom"), 2)
        copies = [
            pltpu.make_async_copy(
                rows_hbm.at[:, pl.ds(pl.multiple_of(part * span, width), width)], out, sem.at[i]
            )
            for i, (part, out) in enumerate(((odd, first), (1 - odd, second)))
        ]
        for copy in copies:
            copy.start()
        for copy in copies:
            copy.wait()

    edge = jax.ShapeDtypeStruct((rows.shape[0], width), rows.dtype)
    first, second = pl.pallas_call(
        kernel,
        out_shape=(edge, edge),
        in_specs=[HBM],
        out_specs=(VMEM, VMEM),
        scratch_shapes=[pltpu.SemaphoreType.DMA((2,))],
        compiler_params=pltpu.CompilerParams(vmem_limit_bytes=8 * 1024 * 1024),
        name="tile_edges",
    )(in_hbm(rows))
    count = lax.axis_size("dom")
    above = [(i, (i + 1 if i % 2 else i - 1) % count) for i in range(count)]
    within = [(i, i - 1 if i % 2 else i + 1) for i in range(count)]
    return lax.ppermute(first, "dom", above), lax.ppermute(second, "dom", within)


def smooth_own(control, corr_offsets, corr_blocks, interp_blocks, perturbations):
    rows, width = control.shape
    blocks, stored, breadth = corr_blocks.shape[:3]
    pairs = blocks // 2
    pair = 2 * breadth
    span = 2 + 2 * HR
    halo = HR * breadth

    def kernel(
        offsets_hbm, control_hbm, corr_hbm, interp_hbm, pert_hbm, out, outer, halo_corr, interp,
        pert, offsets, tile, corr, offsets_sem, tile_sem, corr_sem, later_sem,
    ):
        def tile_copy(c):
            return pltpu.make_async_copy(
                control_hbm.at[:, pl.ds(c * pair, pair)],
                tile.at[:, pl.ds(c * pair, pair)],
                tile_sem.at[c],
            )

        def corr_copies(c):
            copies = []
            for j in range(2):
                b = 2 * c + j
                for s in range(stored):
                    row = pl.multiple_of((offsets[s, b] + HR + j) * breadth, breadth)
                    copies.append(
                        pltpu.make_async_copy(
                            corr_hbm.at[b, s],
                            corr.at[c, pl.ds(row, breadth), pl.ds(j * breadth, breadth)],
                            corr_sem.at[c, j * stored + s],
                        )
                    )
            return copies

        def clear(c):
            zero = jnp.zeros((breadth, breadth), corr.dtype)
            for j in range(2):
                absent = HR + j
                for s in range(stored):
                    absent = absent - offsets[s, 2 * c + j]
                columns = pl.ds(j * breadth, breadth)
                corr[c, pl.ds(pl.multiple_of(absent * breadth, breadth), breadth), columns] = zero
                far = (1 - j) * (span - 1)
                corr[c, far * breadth : (far + 1) * breadth, columns] = zero

        def later_copies(g):
            share = rows // len(stages)
            some = pl.ds(g * share, share)
            count = interp_hbm.shape[0] // len(stages)
            blocks_of = pl.ds(g * count, count)
            return (
                pltpu.make_async_copy(pert_hbm.at[some], pert.at[some], later_sem.at[g, 0]),
                pltpu.make_async_copy(
                    interp_hbm.at[blocks_of], interp.at[blocks_of], later_sem.at[g, 1]
                ),
            )

        stages = [range(sum(STAGES[:g]), sum(STAGES[: g + 1])) for g in range(len(STAGES))]
        offsets_copy = pltpu.make_async_copy(offsets_hbm, offsets, offsets_sem)
        offsets_copy.start()
        tile_ends = [min(stage[-1] + 2, pairs) for stage in stages]
        for c in range(tile_ends[0]):
            tile_copy(c).start()
        offsets_copy.wait()

        @pl.loop(0, pairs)
        def _(c):
            for copy in corr_copies(c):
                copy.start()
            clear(c)

            @pl.when(c == stages[0][-1])
            def _():
                for later in range(tile_ends[0], pairs):
                    tile_copy(later).start()

        for g, stage in enumerate(stages):
            for c in range(tile_ends[g - 1] if g else 0, tile_ends[g]):
                tile_copy(c).wait()
            for c in stage:
                for copy in corr_copies(c):
                    copy.wait()
            if g == 0:
                for h in range(len(stages)):
                    for copy in later_copies(h):
                        copy.start()
            for c in stage:
                first = max(2 * c - HR, 0)
                last = min(2 * c + 2 + HR, blocks)
                start = (first - (2 * c - HR)) * breadth
                depth = (last - first) * breadth
                result = jnp.dot(
                    tile[:, first * breadth : last * breadth],
                    corr[c, start : start + depth, :],
                    preferred_element_type=jnp.float32,
                )
                if c == 0 or c == pairs - 1:
                    side = min(c, 1)
                    outer[side] = result
                    low = side * (span * breadth - halo)
                    halo_corr[side] = corr[c, low : low + halo, :]
                else:
                    result = result.astype(jnp.bfloat16)
                    out[2 * c] = result[:, :breadth]
                    out[2 * c + 1] = result[:, breadth:]
        for g in range(len(stages)):
            for copy in later_copies(g):
                copy.wait()

    return pl.pallas_call(
        kernel,
        out_shape=(
            jax.ShapeDtypeStruct((blocks, rows, breadth), jnp.bfloat16),
            jax.ShapeDtypeStruct((2, rows, pair), jnp.float32),
            jax.ShapeDtypeStruct((2, halo, pair), jnp.bfloat16),
            jax.ShapeDtypeStruct(interp_blocks.shape, jnp.bfloat16),
            jax.ShapeDtypeStruct(perturbations.shape, jnp.bfloat16),
        ),
        in_specs=[HBM] * 5,
        out_specs=(VMEM,) * 5,
        scratch_shapes=[
            pltpu.SMEM((stored, blocks), jnp.int32),
            pltpu.VMEM((rows, width), jnp.bfloat16),
            pltpu.VMEM((pairs, span * breadth, pair), jnp.bfloat16),
            pltpu.SemaphoreType.DMA,
            pltpu.SemaphoreType.DMA((pairs,)),
            pltpu.SemaphoreType.DMA((pairs, 2 * stored)),
            pltpu.SemaphoreType.DMA((len(STAGES), 2)),
        ],
        compiler_params=pltpu.CompilerParams(vmem_limit_bytes=K1_LIMIT * 1024 * 1024),
        cost_estimate=pl.CostEstimate(
            flops=2 * rows * stored * breadth * breadth * blocks,
            bytes_accessed=4 * rows * width,
            transcendentals=0,
        ),
        name="smooth_own",
    )(
        in_hbm(corr_offsets.T), in_hbm(control), in_hbm(corr_blocks), in_hbm(interp_blocks),
        in_hbm(perturbations),
    )


def member_sums(smoothed, interp_index, interp_blocks, perturbations, members, xs, distances, halo=None):
    blocks, rows, breadth = smoothed.shape
    column_blocks, feeding = interp_blocks.shape[:2]
    levels = rows // members
    share = column_blocks // xs

    def kernel(index, interp, pert, *refs):
        outs = refs[-len(distances) :]
        position = lax.axis_index("x")
        if halo is None:
            smooth = refs[0]
        else:
            outer_ref, corr, first_ref, second_ref, smooth = refs[1:6]
            odd = lax.rem(lax.axis_index("dom"), 2)
            for side, halo_ref in ((1 - odd, second_ref), (odd, first_ref)):
                result = outer_ref[side] + jnp.dot(
                    halo_ref[...], corr[side], preferred_element_type=jnp.float32
                )
                result = result.astype(jnp.bfloat16)
                b = side * (blocks - HR)
                smooth[b] = result[:, :breadth]
                smooth[b + 1] = result[:, breadth:]
        for distance, out in zip(distances, outs):
            piece = lax.rem(position + distance, xs)
            for i in range(share):
                q = piece * share + i
                lhs = jnp.concatenate([smooth[index[q, k]] for k in range(feeding)], axis=1)
                spread = jnp.dot(
                    lhs,
                    interp[q].reshape(feeding * breadth, breadth),
                    preferred_element_type=jnp.float32,
                )
                columns = pl.ds(pl.multiple_of(q * breadth, breadth), breadth)
                term = pert[:, columns].astype(jnp.float32) * spread
                total = jnp.sum(term.reshape(members, levels, breadth), axis=0)
                out[:, i * breadth : (i + 1) * breadth] = total.astype(jnp.bfloat16)

    pieces = tuple(
        jax.ShapeDtypeStruct((levels, share * breadth), jnp.bfloat16) for _ in distances
    )
    operands = (interp_blocks, perturbations, smoothed) + (halo or ())
    return pl.pallas_call(
        kernel,
        out_shape=pieces if halo is None else (smoothed,) + pieces,
        in_specs=[VMEM] * (1 + len(operands)),
        out_specs=(VMEM,) * (len(pieces) + (halo is not None)),
        input_output_aliases={} if halo is None else {3: 0},
        compiler_params=pltpu.CompilerParams(vmem_limit_bytes=K2_LIMIT * 1024 * 1024),
        cost_estimate=pl.CostEstimate(
            flops=2 * rows * feeding * breadth * breadth * (share * len(distances) + 1),
            bytes_accessed=6 * rows * share * breadth * len(distances),
            transcendentals=0,
        ),
        name="member_sums",
    )(interp_index, *operands)


def sum_pieces(pieces):
    def kernel(*refs):
        total = refs[0][...].astype(jnp.float32)
        for ref in refs[1:-1]:
            total = total + ref[...].astype(jnp.float32)
        refs[-1][...] = total.astype(jnp.bfloat16)

    return pl.pallas_call(
        kernel,
        out_shape=jax.ShapeDtypeStruct(pieces[0].shape, jnp.bfloat16),
        in_specs=[VMEM] * len(pieces),
        out_specs=VMEM,
        compiler_params=pltpu.CompilerParams(vmem_limit_bytes=8 * 1024 * 1024),
        name="sum_pieces",
    )(*pieces)


def sum_received(parts, factor):
    def kernel(parts_ref, out_ref):
        total = jnp.sum(parts_ref[...].astype(jnp.float32), axis=0) * factor
        out_ref[...] = jnp.broadcast_to(total.astype(jnp.bfloat16)[None], out_ref.shape)

    return pl.pallas_call(
        kernel,
        out_shape=jax.ShapeDtypeStruct(parts.shape, jnp.bfloat16),
        in_specs=[VMEM],
        out_specs=VMEM,
        compiler_params=pltpu.CompilerParams(vmem_limit_bytes=8 * 1024 * 1024),
        name="sum_received",
    )(parts)


def assemble(pieces):
    xs = len(pieces)
    levels, width = pieces[0].shape

    def kernel(*refs):
        refs, out, sem = refs[:xs], refs[xs], refs[xs + 1]
        copies = []
        for k in range(xs):
            x = lax.rem(lax.axis_index("x") + xs - k, xs)
            columns = pl.ds(pl.multiple_of(x * width, width), width)
            copies.append(pltpu.make_async_copy(refs[k], out.at[:, columns], sem.at[k]))
            copies[-1].start()
        for copy in copies:
            copy.wait()

    return pl.pallas_call(
        kernel,
        out_shape=jax.ShapeDtypeStruct((levels, xs * width), jnp.bfloat16),
        in_specs=[VMEM] * xs,
        out_specs=HBM,
        scratch_shapes=[pltpu.SemaphoreType.DMA((xs,))],
        compiler_params=pltpu.CompilerParams(vmem_limit_bytes=8 * 1024 * 1024),
        name="assemble",
    )(*pieces)


def increment(control, corr_offsets, corr_blocks, interp_index, interp_blocks, perturbations):
    members, levels, width = control.shape
    breadth = corr_blocks.shape[2]
    xs = lax.axis_size("x")
    zs = lax.axis_size("z")
    members_all = members * zs * xs
    factor = float(1.0 / (members_all - 1) ** 0.5)
    rows = control.reshape(members * levels, width)
    first, second = tile_halos(rows, HR * breadth)
    smoothed, outer, halo_corr, interp, pert = smooth_own(
        rows, corr_offsets, corr_blocks, interp_blocks,
        perturbations.reshape(members * levels, width),
    )
    pieces = {}
    halo = (outer, halo_corr, first, second)
    for distances in GROUPS:
        results = member_sums(smoothed, interp_index, interp, pert, members, xs, distances, halo)
        if halo:
            smoothed, results, halo = results[0], results[1:], None
        pieces.update(zip(distances, results))

    def along_x(piece, k):
        return lax.ppermute(piece, "x", [(i, (i + k) % xs) for i in range(xs)])

    received = [pieces[0]]
    for k in pieces:
        if k:
            received.append(along_x(pieces[k], k))
    total = sum_pieces(received)
    parts = lax.all_to_all(total.reshape(zs, levels // zs, width // xs), "z", 0, 0)
    column = lax.all_to_all(sum_received(parts, factor), "z", 0, 0)
    column = column.reshape(levels, width // xs)
    return assemble([column] + [along_x(column, k) for k in range(1, xs)])


def solution(mesh):
    zs = 8
    xs = mesh.shape["mem"] // zs
    inner_mesh = jax.sharding.Mesh(
        mesh.devices.reshape(mesh.shape["dom"], zs, xs), ("dom", "z", "x")
    )
    mem = ("z", "x")
    in_specs = (
        P(mem, None, "dom"),
        P("dom", None),
        P("dom", None, None, None),
        P("dom", None),
        P("dom", None, None, None),
        P(mem, None, "dom"),
    )
    out_specs = P(None, "dom")
    return jax.shard_map(
        increment, mesh=inner_mesh, in_specs=in_specs, out_specs=out_specs, check_vma=False
    )
```

time: 277 us -> 65.7 us (0.24)
  waiting for transfers between devices: 160 us -> 11.4 us
  local copies, waits for them, and re-layouts: 59.7 us -> 0.09 us
  blocking collectives: 0 us -> 29.1 us
  matrix products: 25.7 us -> 0 us
  other arithmetic: 15.5 us -> 0 us
  Pallas kernels: 0 us -> 14.4 us
  between operations: 13.4 us -> 0.06 us
  starting transfers between devices: 1.75 us -> 10.4 us
    psum x1 -> x0, waiting for transfers between devices: 154 us -> none  [per_device(): summed = lax.psum(local_sum, 'mem')]
    all_to_all x0 -> x2, blocking collectives: none -> 29.1 us  [the longest x1 17.6 us: increment(): lax.all_to_all(total.reshape(zs, levels // zs, width // xs), 'z', 0, 0)]
    dot_general x2 -> x0, matrix products: 25.7 us -> none  [the longest x1 13.5 us: member_terms(): jnp.einsum('rqkj,qkji->rqi', feeding, interp_blocks, preferred_element_ty...]
    reshape x3 -> x0, local copies, waits for them, and re-layouts: 25.5 us -> none  [the longest x2 16.1 us: smooth_blocks(): tile_rows = extended.reshape(members * levels, blocks + 2 * HR, breadth)]
    gather x2 -> x0, local copies, waits for them, and re-layouts: 20 us -> none  [the longest x1 10.1 us: smooth_blocks(): picked = tile_rows[:, source]]
    pallas_call x0 -> x9, Pallas kernels: none -> 14.4 us  [the longest x1 6.46 us: smooth_own(): pl.pallas_call(kernel, out_shape=(jax.ShapeDtypeStruct((blocks, rows, bre...]
    transpose x1 -> x0, local copies, waits for them, and re-layouts: 11.5 us -> none  [member_terms(): jnp.einsum('rqkj,qkji->rqi', feeding, interp_blocks, preferred_element_ty...]
    ppermute x2 -> x8, starting transfers between devices: 1.75 us -> 10.4 us  [the longest x6 8.29 us: along_x(): return lax.ppermute(piece, 'x', [(i, (i + k) % xs) for i in range(xs)])]
  transfers between devices with their start and end apart: 3 -> 8, of which waited for: 2 -> 6; matrix products, arithmetic and copies ran while one was open for 1% -> 0% of each run, Pallas kernels for 0% -> 12%
where the time goes in v2:
time: 65.7 us; the launch traced here: 65.5 us
  blocking collectives  29.1 us (44%)
  Pallas kernels  14.4 us (22%)
  waiting for transfers between devices  11.4 us (17%)
  starting transfers between devices  10.4 us (16%)
    all_to_all x1, blocking collectives, increment(): lax.all_to_all(total.reshape(zs, levels // zs, width // xs), 'z', 0, 0)  17.6 us
    all_to_all x1, blocking collectives, increment(): column = lax.all_to_all(sum_received(parts, factor), 'z', 0, 0)  11.5 us
    ppermute x6, waiting for transfers between devices, along_x(): return lax.ppermute(piece, 'x', [(i, (i + k) % xs) for i in range(xs)])  11.4 us
    ppermute x6, starting transfers between devices, along_x(): return lax.ppermute(piece, 'x', [(i, (i + k) % xs) for i in range(xs)])  8.29 us
    pallas_call x1, Pallas kernels, smooth_own(): pl.pallas_call(kernel, out_shape=(jax.ShapeDtypeStruct((blocks, rows, bre...  6.46 us
    pallas_call x4, Pallas kernels, member_sums(): pl.pallas_call(kernel, out_shape=pieces if halo is None else (smoothed,)...  5.83 us
    ppermute x1, starting transfers between devices, tile_halos(): lax.ppermute(second, 'dom', within)  1.86 us
  transfers between devices with their start and end apart: 8, of which 6 were waited for; matrix products, arithmetic and copies ran while one was open for 0% of the time, Pallas kernels for 12%

profile of v2, /device:TPU:24, one launch (start us, length us, event | category | flops | bytes accessed | tf_op | source)
XLA Modules:
  0.0 65.5 jit_solution(9857228137627694574)
XLA Ops:
  0.0 0.0 copy-start
  0.0 1.2 %tile_edges.1 = (bf16[1024,256]{1,0:T(8,128)(2,1)S(1)}, bf16[1024,256]{1,0:T(8,128)(2,1)S(1)}) custom-call(bf16[1024,2048]{1,0:T(8,128)(2,1)} %bitcast.10), custom_call_target="tpu_custom_call" | custom-call | tf_op jit(solution)/shard_map/tile_edges/pallas_call | solution.py:38
  1.2 0.3 collective-permute-start
  1.5 1.9 %collective-permute-start.1 = (bf16[1024,256]{1,0:T(8,128)(2,1)S(1)}, bf16[1024,256]{1,0:T(8,128)(2,1)S(1)}, u32[]{:S(2)}, u32[]{:S(2)}) collective-permute-start(bf16[1024,256]{1,0:T(8,128)(2,1)S(1)} %get-tuple-element.20), channel_id=1, source_target_pairs={{0,32},{32,0},{64,96},{96,64},{128,160},{160,128},{192,224},{224,1... | collective-permute-start | bytes 1572872 | tf_op jit(solution)/shard_map/ppermute | solution.py:50
  3.4 0.0 copy-done
  3.4 0.1 copy.9.index
  3.5 6.5 %smooth_own.1 = (bf16[16,1024,128]{2,1,0:T(8,128)(2,1)S(1)}, f32[2,1024,256]{2,1,0:T(8,128)S(1)}, bf16[2,256,256]{2,1,0:T(8,128)(2,1)S(1)}, bf16[16,4,128,128]{3,2,1,0:T(8,128)(2,1)S(1)}, bf16[1024,2048]{1,0:T(8,128)(2,1)S(1)}) custom-call(s32[4,16]{1,0:T(4,128)} %bitcast.13, bf16[1024,2048]{1,0:T(8,128)(2,1)} %bitcast.11, ...), custom_call_target="tpu_custom_call" | custom-call | flops 2147483648 | bytes 8388608 | tf_op jit(solution)/shard_map/smooth_own/pallas_call | solution.py:162
  9.9 0.0 collective-permute-done.refs_3_
  9.9 0.0 collective-permute-done.1.refs_4_
  10.0 1.7 %member_sums.4 = (bf16[16,1024,128]{2,1,0:T(8,128)(2,1)S(1)}, bf16[128,512]{1,0:T(8,128)(2,1)S(1)}) custom-call(s32[16,4]{1,0:T(8,128)S(1)} %copy.9.index, bf16[16,4,128,128]{3,2,1,0:T(8,128)(2,1)S(1)} %get-tuple-element.14.interp, bf16[1024,2048]{1,0:T(8,128)(2,1)S(1)} %get-tuple-element.15.pert, ...), custom_call_target="tpu_custom_call", output_to_operand_aliasing={{0}: (3, {})} | custom-call | flops 671088640 | bytes 3145728 | tf_op jit(solution)/shard_map/member_sums/pallas_call | solution.py:236
  11.6 1.4 %member_sums.7 = bf16[128,512]{1,0:T(8,128)(2,1)S(1)} custom-call(s32[16,4]{1,0:T(8,128)S(1)} %copy.9.index, bf16[16,4,128,128]{3,2,1,0:T(8,128)(2,1)S(1)} %get-tuple-element.14.interp, bf16[1024,2048]{1,0:T(8,128)(2,1)S(1)} %get-tuple-element.15.pert, bf16[16,1024,128]{2,1,0:T(8,128)(2,1)S(1)} %get-tuple-element.21.refs_0_), custom_call_target="tpu_custom_call" | custom-call | flops 671088640 | bytes 3145728 | tf_op jit(solution)/shard_map/member_sums/pallas_call | solution.py:236
  13.0 1.4 %member_sums.6 = bf16[128,512]{1,0:T(8,128)(2,1)S(1)} custom-call(s32[16,4]{1,0:T(8,128)S(1)} %copy.9.index, bf16[16,4,128,128]{3,2,1,0:T(8,128)(2,1)S(1)} %get-tuple-element.14.interp, bf16[1024,2048]{1,0:T(8,128)(2,1)S(1)} %get-tuple-element.15.pert, bf16[16,1024,128]{2,1,0:T(8,128)(2,1)S(1)} %get-tuple-element.21.refs_0_), custom_call_target="tpu_custom_call" | custom-call | flops 671088640 | bytes 3145728 | tf_op jit(solution)/shard_map/member_sums/pallas_call | solution.py:236
  14.4 1.5 %collective-permute-start.3 = (bf16[128,512]{1,0:T(8,128)(2,1)S(1)}, bf16[128,512]{1,0:T(8,128)(2,1)S(1)}, u32[]{:S(2)}, u32[]{:S(2)}) collective-permute-start(bf16[128,512]{1,0:T(8,128)(2,1)S(1)} %member_sums.6), channel_id=1, source_target_pairs={{0,1},{1,2},{2,3},{3,0},{4,5},{5,6},{6,7},{7,4},{8,9},{9,10},{10,1... | collective-permute-start | bytes 393224 | tf_op jit(solution)/shard_map/ppermute | solution.py:332
  16.0 1.8 %collective-permute-start.4 = (bf16[128,512]{1,0:T(8,128)(2,1)S(1)}, bf16[128,512]{1,0:T(8,128)(2,1)S(1)}, u32[]{:S(2)}, u32[]{:S(2)}) collective-permute-start(bf16[128,512]{1,0:T(8,128)(2,1)S(1)} %member_sums.7), channel_id=1, source_target_pairs={{0,3},{1,0},{2,1},{3,2},{4,7},{5,4},{6,5},{7,6},{8,11},{9,8},{10,9... | collective-permute-start | bytes 393224 | tf_op jit(solution)/shard_map/ppermute | solution.py:332
  17.8 1.8 %collective-permute-start.2 = (bf16[128,512]{1,0:T(8,128)(2,1)S(1)}, bf16[128,512]{1,0:T(8,128)(2,1)S(1)}, u32[]{:S(2)}, u32[]{:S(2)}) collective-permute-start(bf16[128,512]{1,0:T(8,128)(2,1)S(1)} %get-tuple-element.22), channel_id=1, source_target_pairs={{0,2},{1,3},{2,0},{3,1},{4,6},{5,7},{6,4},{7,5},{8,10},{9,11},{10,... | collective-permute-start | bytes 393224 | tf_op jit(solution)/shard_map/ppermute | solution.py:332
  19.5 1.4 %member_sums.5.refs_0_ = bf16[128,512]{1,0:T(8,128)(2,1)S(1)} custom-call(s32[16,4]{1,0:T(8,128)S(1)} %copy.9.index, bf16[16,4,128,128]{3,2,1,0:T(8,128)(2,1)S(1)} %get-tuple-element.14.interp, bf16[1024,2048]{1,0:T(8,128)(2,1)S(1)} %get-tuple-element.15.pert, bf16[16,1024,128]{2,1,0:T(8,128)(2,1)S(1)} %get-tuple-element.21.refs_0_), custom_call_target="tpu_custom_call" | custom-call | flops 671088640 | bytes 3145728 | tf_op jit(solution)/shard_map/member_sums/pallas_call | solution.py:236
  20.9 1.2 %collective-permute-done.3.refs_2_ = bf16[128,512]{1,0:T(8,128)(2,1)S(1)} collective-permute-done((bf16[128,512]{1,0:T(8,128)(2,1)S(1)}, bf16[128,512]{1,0:T(8,128)(2,1)S(1)}, u32[]{:S(2)}, u32[]{:S(2)}) %collective-permute-start.3) | collective-permute-done | bytes 131104 | tf_op jit(solution)/shard_map/ppermute | solution.py:332
  22.1 2.2 %collective-permute-done.4.refs_3_ = bf16[128,512]{1,0:T(8,128)(2,1)S(1)} collective-permute-done((bf16[128,512]{1,0:T(8,128)(2,1)S(1)}, bf16[128,512]{1,0:T(8,128)(2,1)S(1)}, u32[]{:S(2)}, u32[]{:S(2)}) %collective-permute-start.4) | collective-permute-done | bytes 131104 | tf_op jit(solution)/shard_map/ppermute | solution.py:332
  24.2 1.5 %collective-permute-done.2.refs_1_ = bf16[128,512]{1,0:T(8,128)(2,1)S(1)} collective-permute-done((bf16[128,512]{1,0:T(8,128)(2,1)S(1)}, bf16[128,512]{1,0:T(8,128)(2,1)S(1)}, u32[]{:S(2)}, u32[]{:S(2)}) %collective-permute-start.2) | collective-permute-done | bytes 131104 | tf_op jit(solution)/shard_map/ppermute | solution.py:332
  25.8 0.1 sum_pieces.1
  25.9 17.6 %all_to_all.10.parts_ref = bf16[8,16,512]{2,1,0:T(8,128)(2,1)S(1)} all-to-all(bf16[8,16,512]{2,1,0:T(8,128)(2,1)S(1)} %bitcast.5), channel_id=1, replica_groups=mesh['dom'=8,'z'=8,'x'=4] {'z'}, dimensions={0} | all-to-all | bytes 262144 | tf_op jit(solution)/shard_map/all_to_all | solution.py:339
  43.5 11.5 %all_to_all.11 = bf16[8,16,512]{2,1,0:T(8,128)(2,1)S(1)} all-to-all(bf16[8,16,512]{2,1,0:T(8,128)(2,1)S(1)} %sum_received.1), channel_id=1, replica_groups=mesh['dom'=8,'z'=8,'x'=4] {'z'}, dimensions={0} | all-to-all | bytes 262144 | tf_op jit(solution)/shard_map/all_to_all | solution.py:340
  54.9 1.9 %collective-permute-start.7 = (bf16[128,512]{1,0:T(8,128)(2,1)S(1)}, bf16[128,512]{1,0:T(8,128)(2,1)S(1)}, u32[]{:S(2)}, u32[]{:S(2)}) collective-permute-start(bf16[128,512]{1,0:T(8,128)(2,1)S(1)} %bitcast.6), channel_id=1, source_target_pairs={{0,3},{1,0},{2,1},{3,2},{4,7},{5,4},{6,5},{7,6},{8,11},{9,8},{10,9... | collective-permute-start | bytes 393224 | tf_op jit(solution)/shard_map/ppermute | solution.py:332
  56.8 1.3 %collective-permute-start.6 = (bf16[128,512]{1,0:T(8,128)(2,1)S(1)}, bf16[128,512]{1,0:T(8,128)(2,1)S(1)}, u32[]{:S(2)}, u32[]{:S(2)}) collective-permute-start(bf16[128,512]{1,0:T(8,128)(2,1)S(1)} %bitcast.7), channel_id=1, source_target_pairs={{0,2},{1,3},{2,0},{3,1},{4,6},{5,7},{6,4},{7,5},{8,10},{9,11},{10,... | collective-permute-start | bytes 393224 | tf_op jit(solution)/shard_map/ppermute | solution.py:332
  58.1 0.0 collective-permute-start.5
  58.1 2.6 %collective-permute-done.7.refs_3_ = bf16[128,512]{1,0:T(8,128)(2,1)S(1)} collective-permute-done((bf16[128,512]{1,0:T(8,128)(2,1)S(1)}, bf16[128,512]{1,0:T(8,128)(2,1)S(1)}, u32[]{:S(2)}, u32[]{:S(2)}) %collective-permute-start.7) | collective-permute-done | bytes 131104 | tf_op jit(solution)/shard_map/ppermute | solution.py:332
  60.7 2.6 %collective-permute-done.6.refs_2_ = bf16[128,512]{1,0:T(8,128)(2,1)S(1)} collective-permute-done((bf16[128,512]{1,0:T(8,128)(2,1)S(1)}, bf16[128,512]{1,0:T(8,128)(2,1)S(1)}, u32[]{:S(2)}, u32[]{:S(2)}) %collective-permute-start.6) | collective-permute-done | bytes 131104 | tf_op jit(solution)/shard_map/ppermute | solution.py:332
  63.3 1.4 %collective-permute-done.5.refs_1_ = bf16[128,512]{1,0:T(8,128)(2,1)S(1)} collective-permute-done((bf16[128,512]{1,0:T(8,128)(2,1)S(1)}, bf16[128,512]{1,0:T(8,128)(2,1)S(1)}, u32[]{:S(2)}, u32[]{:S(2)}) %collective-permute-start.5) | collective-permute-done | bytes 131104 | tf_op jit(solution)/shard_map/ppermute | solution.py:332
  64.7 0.8 %assemble.1 = bf16[128,2048]{1,0:T(8,128)(2,1)} custom-call(bf16[128,512]{1,0:T(8,128)(2,1)S(1)} %bitcast.9, bf16[128,512]{1,0:T(8,128)(2,1)S(1)} %collective-permute-done.5.refs_1_, bf16[128,512]{1,0:T(8,128)(2,1)S(1)} %collective-permute-done.6.refs_2_, bf16[128,512]{1,0:T(8,128)(2,1)S(1)} %collective-permute-done.7.refs_3_), custom_call_target="tpu_custom_call" | custom-call | tf_op jit(solution)/shard_map/assemble/pallas_call | solution.py:299
  (1 shorter events, 0.0 us)
Async XLA Ops:
  0.0 3.4 %copy-start = (s32[16,4]{0,1:T(4,128)S(1)}, s32[16,4]{0,1:T(4,128)}, u32[]{:S(2)}) copy-start(s32[16,4]{0,1:T(4,128)} %param.9) | copy-start | bytes 772
  1.2 8.7 %collective-permute-start = (bf16[1024,256]{1,0:T(8,128)(2,1)S(1)}, bf16[1024,256]{1,0:T(8,128)(2,1)S(1)}, u32[]{:S(2)}, u32[]{:S(2)}) collective-permute-start(bf16[1024,256]{1,0:T(8,128)(2,1)S(1)} %get-tuple-element.19), channel_id=1, source_target_pairs={{0,224},{32,64},{64,32},{96,128},{128,96},{160,192},{192,160},{224... | collective-permute-start | bytes 1572872 | tf_op jit(solution)/shard_map/ppermute | solution.py:50
  1.5 8.4 %collective-permute-start.1 = (bf16[1024,256]{1,0:T(8,128)(2,1)S(1)}, bf16[1024,256]{1,0:T(8,128)(2,1)S(1)}, u32[]{:S(2)}, u32[]{:S(2)}) collective-permute-start(bf16[1024,256]{1,0:T(8,128)(2,1)S(1)} %get-tuple-element.20), channel_id=1, source_target_pairs={{0,32},{32,0},{64,96},{96,64},{128,160},{160,128},{192,224},{224,1... | collective-permute-start | bytes 1572872 | tf_op jit(solution)/shard_map/ppermute | solution.py:50
  14.4 7.6 %collective-permute-start.3 = (bf16[128,512]{1,0:T(8,128)(2,1)S(1)}, bf16[128,512]{1,0:T(8,128)(2,1)S(1)}, u32[]{:S(2)}, u32[]{:S(2)}) collective-permute-start(bf16[128,512]{1,0:T(8,128)(2,1)S(1)} %member_sums.6), channel_id=1, source_target_pairs={{0,1},{1,2},{2,3},{3,0},{4,5},{5,6},{6,7},{7,4},{8,9},{9,10},{10,1... | collective-permute-start | bytes 393224 | tf_op jit(solution)/shard_map/ppermute | solution.py:332
  16.0 8.3 %collective-permute-start.4 = (bf16[128,512]{1,0:T(8,128)(2,1)S(1)}, bf16[128,512]{1,0:T(8,128)(2,1)S(1)}, u32[]{:S(2)}, u32[]{:S(2)}) collective-permute-start(bf16[128,512]{1,0:T(8,128)(2,1)S(1)} %member_sums.7), channel_id=1, source_target_pairs={{0,3},{1,0},{2,1},{3,2},{4,7},{5,4},{6,5},{7,6},{8,11},{9,8},{10,9... | collective-permute-start | bytes 393224 | tf_op jit(solution)/shard_map/ppermute | solution.py:332
  17.8 8.0 %collective-permute-start.2 = (bf16[128,512]{1,0:T(8,128)(2,1)S(1)}, bf16[128,512]{1,0:T(8,128)(2,1)S(1)}, u32[]{:S(2)}, u32[]{:S(2)}) collective-permute-start(bf16[128,512]{1,0:T(8,128)(2,1)S(1)} %get-tuple-element.22), channel_id=1, source_target_pairs={{0,2},{1,3},{2,0},{3,1},{4,6},{5,7},{6,4},{7,5},{8,10},{9,11},{10,... | collective-permute-start | bytes 393224 | tf_op jit(solution)/shard_map/ppermute | solution.py:332
  54.9 5.8 %collective-permute-start.7 = (bf16[128,512]{1,0:T(8,128)(2,1)S(1)}, bf16[128,512]{1,0:T(8,128)(2,1)S(1)}, u32[]{:S(2)}, u32[]{:S(2)}) collective-permute-start(bf16[128,512]{1,0:T(8,128)(2,1)S(1)} %bitcast.6), channel_id=1, source_target_pairs={{0,3},{1,0},{2,1},{3,2},{4,7},{5,4},{6,5},{7,6},{8,11},{9,8},{10,9... | collective-permute-start | bytes 393224 | tf_op jit(solution)/shard_map/ppermute | solution.py:332
  56.8 6.5 %collective-permute-start.6 = (bf16[128,512]{1,0:T(8,128)(2,1)S(1)}, bf16[128,512]{1,0:T(8,128)(2,1)S(1)}, u32[]{:S(2)}, u32[]{:S(2)}) collective-permute-start(bf16[128,512]{1,0:T(8,128)(2,1)S(1)} %bitcast.7), channel_id=1, source_target_pairs={{0,2},{1,3},{2,0},{3,1},{4,6},{5,7},{6,4},{7,5},{8,10},{9,11},{10,... | collective-permute-start | bytes 393224 | tf_op jit(solution)/shard_map/ppermute | solution.py:332
  58.1 6.6 %collective-permute-start.5 = (bf16[128,512]{1,0:T(8,128)(2,1)S(1)}, bf16[128,512]{1,0:T(8,128)(2,1)S(1)}, u32[]{:S(2)}, u32[]{:S(2)}) collective-permute-start(bf16[128,512]{1,0:T(8,128)(2,1)S(1)} %bitcast.8), channel_id=1, source_target_pairs={{0,1},{1,2},{2,3},{3,0},{4,5},{5,6},{6,7},{7,4},{8,9},{9,10},{10,1... | collective-permute-start | bytes 393224 | tf_op jit(solution)/shard_map/ppermute | solution.py:332

commit v3 on v2

--- a/solution.py
+++ b/solution.py
@@ -6,8 +6,9 @@
 from jax.sharding import PartitionSpec as P
 
 HR = 2
-GROUPS = ((2,), (1,), (3,), (0,))
+GROUPS = ((2,), (3,), (1,), (0,))
 STAGES = (2, 6)
+LATER = 0
 K1_LIMIT = 24
 K2_LIMIT = 24
 HBM = pl.BlockSpec(memory_space=pltpu.HBM)
@@ -60,37 +61,28 @@
 
     def kernel(
         offsets_hbm, control_hbm, corr_hbm, interp_hbm, pert_hbm, out, outer, halo_corr, interp,
-        pert, offsets, tile, corr, offsets_sem, tile_sem, corr_sem, later_sem,
+        pert, offsets, tile, held, corr, offsets_sem, tile_sem, corr_sem, later_sem,
     ):
         def tile_copy(c):
+            columns = pl.ds(pl.multiple_of(c * pair, pair), pair)
             return pltpu.make_async_copy(
-                control_hbm.at[:, pl.ds(c * pair, pair)],
-                tile.at[:, pl.ds(c * pair, pair)],
-                tile_sem.at[c],
+                control_hbm.at[:, columns], tile.at[:, columns], tile_sem.at[c]
             )
 
-        def corr_copies(c):
-            copies = []
-            for j in range(2):
-                b = 2 * c + j
-                for s in range(stored):
-                    row = pl.multiple_of((offsets[s, b] + HR + j) * breadth, breadth)
-                    copies.append(
-                        pltpu.make_async_copy(
-                            corr_hbm.at[b, s],
-                            corr.at[c, pl.ds(row, breadth), pl.ds(j * breadth, breadth)],
-                            corr_sem.at[c, j * stored + s],
-                        )
-                    )
-            return copies
-
-        def clear(c):
+        def stored_copy(c):
+            both = pl.ds(2 * c, 2)
+            return pltpu.make_async_copy(corr_hbm.at[both], held.at[both], corr_sem.at[c])
+
+        def lay_out(c):
             zero = jnp.zeros((breadth, breadth), corr.dtype)
             for j in range(2):
+                columns = pl.ds(j * breadth, breadth)
                 absent = HR + j
                 for s in range(stored):
-                    absent = absent - offsets[s, 2 * c + j]
-                columns = pl.ds(j * breadth, breadth)
+                    offset = offsets[s, 2 * c + j]
+                    absent = absent - offset
+                    row = pl.multiple_of((offset + HR + j) * breadth, breadth)
+                    corr[c, pl.ds(row, breadth), columns] = held[2 * c + j, s]
                 corr[c, pl.ds(pl.multiple_of(absent * breadth, breadth), breadth), columns] = zero
                 far = (1 - j) * (span - 1)
                 corr[c, far * breadth : (far + 1) * breadth, columns] = zero
@@ -111,28 +103,26 @@
         offsets_copy = pltpu.make_async_copy(offsets_hbm, offsets, offsets_sem)
         offsets_copy.start()
         tile_ends = [min(stage[-1] + 2, pairs) for stage in stages]
-        for c in range(tile_ends[0]):
-            tile_copy(c).start()
-        offsets_copy.wait()
-
-        @pl.loop(0, pairs)
-        def _(c):
-            for copy in corr_copies(c):
-                copy.start()
-            clear(c)
-
-            @pl.when(c == stages[0][-1])
-            def _():
-                for later in range(tile_ends[0], pairs):
-                    tile_copy(later).start()
-
         for g, stage in enumerate(stages):
+
+            @pl.loop(tile_ends[g - 1] if g else 0, tile_ends[g])
+            def _(c):
+                tile_copy(c).start()
+
+            @pl.loop(stage[0], stage[-1] + 1)
+            def _(c):
+                stored_copy(c).start()
+
+        for g, stage in enumerate(stages):
+            for c in stage:
+                stored_copy(c).wait()
+            if g == 0:
+                offsets_copy.wait()
+            for c in stage:
+                lay_out(c)
             for c in range(tile_ends[g - 1] if g else 0, tile_ends[g]):
                 tile_copy(c).wait()
-            for c in stage:
-                for copy in corr_copies(c):
-                    copy.wait()
-            if g == 0:
+            if g == LATER:
                 for h in range(len(stages)):
                     for copy in later_copies(h):
                         copy.start()
@@ -173,10 +163,11 @@
         scratch_shapes=[
             pltpu.SMEM((stored, blocks), jnp.int32),
             pltpu.VMEM((rows, width), jnp.bfloat16),
+            pltpu.VMEM(corr_blocks.shape, jnp.bfloat16),
             pltpu.VMEM((pairs, span * breadth, pair), jnp.bfloat16),
             pltpu.SemaphoreType.DMA,
             pltpu.SemaphoreType.DMA((pairs,)),
-            pltpu.SemaphoreType.DMA((pairs, 2 * stored)),
+            pltpu.SemaphoreType.DMA((pairs,)),
             pltpu.SemaphoreType.DMA((len(STAGES), 2)),
         ],
         compiler_params=pltpu.CompilerParams(vmem_limit_bytes=K1_LIMIT * 1024 * 1024),

time: 65.7 us -> 65.6 us (level)
  waiting for transfers between devices: 11.4 us -> 13.2 us
  starting transfers between devices: 10.4 us -> 9.28 us
    ppermute x6, waiting for transfers between devices: 11.4 us -> 12.7 us  [along_x(): return lax.ppermute(piece, 'x', [(i, (i + k) % xs) for i in range(xs)])]
    ppermute x6, starting transfers between devices: 8.29 us -> 7.15 us  [along_x(): return lax.ppermute(piece, 'x', [(i, (i + k) % xs) for i in range(xs)])]
  transfers between devices with their start and end apart: 8 -> 8, of which waited for: 6 -> 6; matrix products, arithmetic and copies ran while one was open for 0% -> 0% of each run, Pallas kernels for 12% -> 11%
where the time goes in v3:
time: 65.6 us; the launch traced here: 65.5 us
  blocking collectives  28.9 us (44%)
  Pallas kernels  14 us (21%)
  waiting for transfers between devices  13.2 us (20%)
  starting transfers between devices  9.28 us (14%)
    all_to_all x1, blocking collectives, increment(): lax.all_to_all(total.reshape(zs, levels // zs, width // xs), 'z', 0, 0)  17.4 us
    ppermute x6, waiting for transfers between devices, along_x(): return lax.ppermute(piece, 'x', [(i, (i + k) % xs) for i in range(xs)])  12.7 us
    all_to_all x1, blocking collectives, increment(): column = lax.all_to_all(sum_received(parts, factor), 'z', 0, 0)  11.5 us
    ppermute x6, starting transfers between devices, along_x(): return lax.ppermute(piece, 'x', [(i, (i + k) % xs) for i in range(xs)])  7.15 us
    pallas_call x1, Pallas kernels, smooth_own(): pl.pallas_call(kernel, out_shape=(jax.ShapeDtypeStruct((blocks, rows, bre...  6.02 us
    pallas_call x4, Pallas kernels, member_sums(): pl.pallas_call(kernel, out_shape=pieces if halo is None else (smoothed,)...  5.81 us
    ppermute x1, starting transfers between devices, tile_halos(): lax.ppermute(second, 'dom', within)  1.86 us
  transfers between devices with their start and end apart: 8, of which 6 were waited for; matrix products, arithmetic and copies ran while one was open for 0% of the time, Pallas kernels for 11%

profile of v3, /device:TPU:24, one launch (start us, length us, event | category | flops | bytes accessed | tf_op | source)
XLA Modules:
  0.0 65.5 jit_solution(11666437175087043757)
XLA Ops:
  0.0 0.0 copy-start
  0.0 1.2 %tile_edges.1 = (bf16[1024,256]{1,0:T(8,128)(2,1)S(1)}, bf16[1024,256]{1,0:T(8,128)(2,1)S(1)}) custom-call(bf16[1024,2048]{1,0:T(8,128)(2,1)} %bitcast.10), custom_call_target="tpu_custom_call" | custom-call | tf_op jit(solution)/shard_map/tile_edges/pallas_call | solution.py:39
  1.2 0.3 collective-permute-start
  1.5 1.9 %collective-permute-start.1 = (bf16[1024,256]{1,0:T(8,128)(2,1)S(1)}, bf16[1024,256]{1,0:T(8,128)(2,1)S(1)}, u32[]{:S(2)}, u32[]{:S(2)}) collective-permute-start(bf16[1024,256]{1,0:T(8,128)(2,1)S(1)} %get-tuple-element.20), channel_id=1, source_target_pairs={{0,32},{32,0},{64,96},{96,64},{128,160},{160,128},{192,224},{224,1... | collective-permute-start | bytes 1572872 | tf_op jit(solution)/shard_map/ppermute | solution.py:51
  3.4 0.0 copy-done
  3.4 0.1 copy.9.index
  3.5 6.0 %smooth_own.1 = (bf16[16,1024,128]{2,1,0:T(8,128)(2,1)S(1)}, f32[2,1024,256]{2,1,0:T(8,128)S(1)}, bf16[2,256,256]{2,1,0:T(8,128)(2,1)S(1)}, bf16[16,4,128,128]{3,2,1,0:T(8,128)(2,1)S(1)}, bf16[1024,2048]{1,0:T(8,128)(2,1)S(1)}) custom-call(s32[4,16]{1,0:T(4,128)} %bitcast.13, bf16[1024,2048]{1,0:T(8,128)(2,1)} %bitcast.11, ...), custom_call_target="tpu_custom_call" | custom-call | flops 2147483648 | bytes 8388608 | tf_op jit(solution)/shard_map/smooth_own/pallas_call | solution.py:152
  9.5 0.4 collective-permute-done.refs_3_
  9.9 0.0 collective-permute-done.1.refs_4_
  9.9 1.7 %member_sums.4 = (bf16[16,1024,128]{2,1,0:T(8,128)(2,1)S(1)}, bf16[128,512]{1,0:T(8,128)(2,1)S(1)}) custom-call(s32[16,4]{1,0:T(8,128)S(1)} %copy.9.index, bf16[16,4,128,128]{3,2,1,0:T(8,128)(2,1)S(1)} %get-tuple-element.14.interp, bf16[1024,2048]{1,0:T(8,128)(2,1)S(1)} %get-tuple-element.15.pert, ...), custom_call_target="tpu_custom_call", output_to_operand_aliasing={{0}: (3, {})} | custom-call | flops 671088640 | bytes 3145728 | tf_op jit(solution)/shard_map/member_sums/pallas_call | solution.py:227
  11.6 1.4 %member_sums.7 = bf16[128,512]{1,0:T(8,128)(2,1)S(1)} custom-call(s32[16,4]{1,0:T(8,128)S(1)} %copy.9.index, bf16[16,4,128,128]{3,2,1,0:T(8,128)(2,1)S(1)} %get-tuple-element.14.interp, bf16[1024,2048]{1,0:T(8,128)(2,1)S(1)} %get-tuple-element.15.pert, bf16[16,1024,128]{2,1,0:T(8,128)(2,1)S(1)} %get-tuple-element.21.refs_0_), custom_call_target="tpu_custom_call" | custom-call | flops 671088640 | bytes 3145728 | tf_op jit(solution)/shard_map/member_sums/pallas_call | solution.py:227
  13.0 1.4 %member_sums.6 = bf16[128,512]{1,0:T(8,128)(2,1)S(1)} custom-call(s32[16,4]{1,0:T(8,128)S(1)} %copy.9.index, bf16[16,4,128,128]{3,2,1,0:T(8,128)(2,1)S(1)} %get-tuple-element.14.interp, bf16[1024,2048]{1,0:T(8,128)(2,1)S(1)} %get-tuple-element.15.pert, bf16[16,1024,128]{2,1,0:T(8,128)(2,1)S(1)} %get-tuple-element.21.refs_0_), custom_call_target="tpu_custom_call" | custom-call | flops 671088640 | bytes 3145728 | tf_op jit(solution)/shard_map/member_sums/pallas_call | solution.py:227
  14.4 2.8 %collective-permute-start.3 = (bf16[128,512]{1,0:T(8,128)(2,1)S(1)}, bf16[128,512]{1,0:T(8,128)(2,1)S(1)}, u32[]{:S(2)}, u32[]{:S(2)}) collective-permute-start(bf16[128,512]{1,0:T(8,128)(2,1)S(1)} %member_sums.6), channel_id=1, source_target_pairs={{0,3},{1,0},{2,1},{3,2},{4,7},{5,4},{6,5},{7,6},{8,11},{9,8},{10,9... | collective-permute-start | bytes 393224 | tf_op jit(solution)/shard_map/ppermute | solution.py:323
  17.2 0.0 collective-permute-start.4
  17.2 2.3 %collective-permute-start.2 = (bf16[128,512]{1,0:T(8,128)(2,1)S(1)}, bf16[128,512]{1,0:T(8,128)(2,1)S(1)}, u32[]{:S(2)}, u32[]{:S(2)}) collective-permute-start(bf16[128,512]{1,0:T(8,128)(2,1)S(1)} %get-tuple-element.22), channel_id=1, source_target_pairs={{0,2},{1,3},{2,0},{3,1},{4,6},{5,7},{6,4},{7,5},{8,10},{9,11},{10,... | collective-permute-start | bytes 393224 | tf_op jit(solution)/shard_map/ppermute | solution.py:323
  19.5 1.4 %member_sums.5.refs_0_ = bf16[128,512]{1,0:T(8,128)(2,1)S(1)} custom-call(s32[16,4]{1,0:T(8,128)S(1)} %copy.9.index, bf16[16,4,128,128]{3,2,1,0:T(8,128)(2,1)S(1)} %get-tuple-element.14.interp, bf16[1024,2048]{1,0:T(8,128)(2,1)S(1)} %get-tuple-element.15.pert, bf16[16,1024,128]{2,1,0:T(8,128)(2,1)S(1)} %get-tuple-element.21.refs_0_), custom_call_target="tpu_custom_call" | custom-call | flops 671088640 | bytes 3145728 | tf_op jit(solution)/shard_map/member_sums/pallas_call | solution.py:227
  20.9 0.1 collective-permute-done.3.refs_2_
  21.0 6.4 %collective-permute-done.4.refs_3_ = bf16[128,512]{1,0:T(8,128)(2,1)S(1)} collective-permute-done((bf16[128,512]{1,0:T(8,128)(2,1)S(1)}, bf16[128,512]{1,0:T(8,128)(2,1)S(1)}, u32[]{:S(2)}, u32[]{:S(2)}) %collective-permute-start.4) | collective-permute-done | bytes 131104 | tf_op jit(solution)/shard_map/ppermute | solution.py:323
  27.4 0.0 collective-permute-done.2.refs_1_
  27.4 0.1 sum_pieces.1
  27.5 17.4 %all_to_all.10.parts_ref = bf16[8,16,512]{2,1,0:T(8,128)(2,1)S(1)} all-to-all(bf16[8,16,512]{2,1,0:T(8,128)(2,1)S(1)} %bitcast.5), channel_id=1, replica_groups=mesh['dom'=8,'z'=8,'x'=4] {'z'}, dimensions={0} | all-to-all | bytes 262144 | tf_op jit(solution)/shard_map/all_to_all | solution.py:330
  45.0 11.5 %all_to_all.11 = bf16[8,16,512]{2,1,0:T(8,128)(2,1)S(1)} all-to-all(bf16[8,16,512]{2,1,0:T(8,128)(2,1)S(1)} %sum_received.1), channel_id=1, replica_groups=mesh['dom'=8,'z'=8,'x'=4] {'z'}, dimensions={0} | all-to-all | bytes 262144 | tf_op jit(solution)/shard_map/all_to_all | solution.py:331
  56.4 0.3 collective-permute-start.7
  56.8 0.5 collective-permute-start.6
  57.3 1.2 %collective-permute-start.5 = (bf16[128,512]{1,0:T(8,128)(2,1)S(1)}, bf16[128,512]{1,0:T(8,128)(2,1)S(1)}, u32[]{:S(2)}, u32[]{:S(2)}) collective-permute-start(bf16[128,512]{1,0:T(8,128)(2,1)S(1)} %bitcast.8), channel_id=1, source_target_pairs={{0,1},{1,2},{2,3},{3,0},{4,5},{5,6},{6,7},{7,4},{8,9},{9,10},{10,1... | collective-permute-start | bytes 393224 | tf_op jit(solution)/shard_map/ppermute | solution.py:323
  58.5 2.9 %collective-permute-done.7.refs_3_ = bf16[128,512]{1,0:T(8,128)(2,1)S(1)} collective-permute-done((bf16[128,512]{1,0:T(8,128)(2,1)S(1)}, bf16[128,512]{1,0:T(8,128)(2,1)S(1)}, u32[]{:S(2)}, u32[]{:S(2)}) %collective-permute-start.7) | collective-permute-done | bytes 131104 | tf_op jit(solution)/shard_map/ppermute | solution.py:323
  61.4 1.9 %collective-permute-done.6.refs_2_ = bf16[128,512]{1,0:T(8,128)(2,1)S(1)} collective-permute-done((bf16[128,512]{1,0:T(8,128)(2,1)S(1)}, bf16[128,512]{1,0:T(8,128)(2,1)S(1)}, u32[]{:S(2)}, u32[]{:S(2)}) %collective-permute-start.6) | collective-permute-done | bytes 131104 | tf_op jit(solution)/shard_map/ppermute | solution.py:323
  63.3 1.3 %collective-permute-done.5.refs_1_ = bf16[128,512]{1,0:T(8,128)(2,1)S(1)} collective-permute-done((bf16[128,512]{1,0:T(8,128)(2,1)S(1)}, bf16[128,512]{1,0:T(8,128)(2,1)S(1)}, u32[]{:S(2)}, u32[]{:S(2)}) %collective-permute-start.5) | collective-permute-done | bytes 131104 | tf_op jit(solution)/shard_map/ppermute | solution.py:323
  64.7 0.8 %assemble.1 = bf16[128,2048]{1,0:T(8,128)(2,1)} custom-call(bf16[128,512]{1,0:T(8,128)(2,1)S(1)} %bitcast.9, bf16[128,512]{1,0:T(8,128)(2,1)S(1)} %collective-permute-done.5.refs_1_, bf16[128,512]{1,0:T(8,128)(2,1)S(1)} %collective-permute-done.6.refs_2_, bf16[128,512]{1,0:T(8,128)(2,1)S(1)} %collective-permute-done.7.refs_3_), custom_call_target="tpu_custom_call" | custom-call | tf_op jit(solution)/shard_map/assemble/pallas_call | solution.py:290
  (1 shorter events, 0.0 us)
Async XLA Ops:
  0.0 3.4 %copy-start = (s32[16,4]{0,1:T(4,128)S(1)}, s32[16,4]{0,1:T(4,128)}, u32[]{:S(2)}) copy-start(s32[16,4]{0,1:T(4,128)} %param.9) | copy-start | bytes 772
  1.2 8.7 %collective-permute-start = (bf16[1024,256]{1,0:T(8,128)(2,1)S(1)}, bf16[1024,256]{1,0:T(8,128)(2,1)S(1)}, u32[]{:S(2)}, u32[]{:S(2)}) collective-permute-start(bf16[1024,256]{1,0:T(8,128)(2,1)S(1)} %get-tuple-element.19), channel_id=1, source_target_pairs={{0,224},{32,64},{64,32},{96,128},{128,96},{160,192},{192,160},{224... | collective-permute-start | bytes 1572872 | tf_op jit(solution)/shard_map/ppermute | solution.py:51
  1.5 8.4 %collective-permute-start.1 = (bf16[1024,256]{1,0:T(8,128)(2,1)S(1)}, bf16[1024,256]{1,0:T(8,128)(2,1)S(1)}, u32[]{:S(2)}, u32[]{:S(2)}) collective-permute-start(bf16[1024,256]{1,0:T(8,128)(2,1)S(1)} %get-tuple-element.20), channel_id=1, source_target_pairs={{0,32},{32,0},{64,96},{96,64},{128,160},{160,128},{192,224},{224,1... | collective-permute-start | bytes 1572872 | tf_op jit(solution)/shard_map/ppermute | solution.py:51
  14.4 6.6 %collective-permute-start.3 = (bf16[128,512]{1,0:T(8,128)(2,1)S(1)}, bf16[128,512]{1,0:T(8,128)(2,1)S(1)}, u32[]{:S(2)}, u32[]{:S(2)}) collective-permute-start(bf16[128,512]{1,0:T(8,128)(2,1)S(1)} %member_sums.6), channel_id=1, source_target_pairs={{0,3},{1,0},{2,1},{3,2},{4,7},{5,4},{6,5},{7,6},{8,11},{9,8},{10,9... | collective-permute-start | bytes 393224 | tf_op jit(solution)/shard_map/ppermute | solution.py:323
  17.2 10.2 %collective-permute-start.4 = (bf16[128,512]{1,0:T(8,128)(2,1)S(1)}, bf16[128,512]{1,0:T(8,128)(2,1)S(1)}, u32[]{:S(2)}, u32[]{:S(2)}) collective-permute-start(bf16[128,512]{1,0:T(8,128)(2,1)S(1)} %member_sums.7), channel_id=1, source_target_pairs={{0,1},{1,2},{2,3},{3,0},{4,5},{5,6},{6,7},{7,4},{8,9},{9,10},{10,1... | collective-permute-start | bytes 393224 | tf_op jit(solution)/shard_map/ppermute | solution.py:323
  17.2 10.2 %collective-permute-start.2 = (bf16[128,512]{1,0:T(8,128)(2,1)S(1)}, bf16[128,512]{1,0:T(8,128)(2,1)S(1)}, u32[]{:S(2)}, u32[]{:S(2)}) collective-permute-start(bf16[128,512]{1,0:T(8,128)(2,1)S(1)} %get-tuple-element.22), channel_id=1, source_target_pairs={{0,2},{1,3},{2,0},{3,1},{4,6},{5,7},{6,4},{7,5},{8,10},{9,11},{10,... | collective-permute-start | bytes 393224 | tf_op jit(solution)/shard_map/ppermute | solution.py:323
  56.4 5.0 %collective-permute-start.7 = (bf16[128,512]{1,0:T(8,128)(2,1)S(1)}, bf16[128,512]{1,0:T(8,128)(2,1)S(1)}, u32[]{:S(2)}, u32[]{:S(2)}) collective-permute-start(bf16[128,512]{1,0:T(8,128)(2,1)S(1)} %bitcast.6), channel_id=1, source_target_pairs={{0,3},{1,0},{2,1},{3,2},{4,7},{5,4},{6,5},{7,6},{8,11},{9,8},{10,9... | collective-permute-start | bytes 393224 | tf_op jit(solution)/shard_map/ppermute | solution.py:323
  56.8 6.5 %collective-permute-start.6 = (bf16[128,512]{1,0:T(8,128)(2,1)S(1)}, bf16[128,512]{1,0:T(8,128)(2,1)S(1)}, u32[]{:S(2)}, u32[]{:S(2)}) collective-permute-start(bf16[128,512]{1,0:T(8,128)(2,1)S(1)} %bitcast.7), channel_id=1, source_target_pairs={{0,2},{1,3},{2,0},{3,1},{4,6},{5,7},{6,4},{7,5},{8,10},{9,11},{10,... | collective-permute-start | bytes 393224 | tf_op jit(solution)/shard_map/ppermute | solution.py:323
  57.3 7.4 %collective-permute-start.5 = (bf16[128,512]{1,0:T(8,128)(2,1)S(1)}, bf16[128,512]{1,0:T(8,128)(2,1)S(1)}, u32[]{:S(2)}, u32[]{:S(2)}) collective-permute-start(bf16[128,512]{1,0:T(8,128)(2,1)S(1)} %bitcast.8), channel_id=1, source_target_pairs={{0,1},{1,2},{2,3},{3,0},{4,5},{5,6},{6,7},{7,4},{8,9},{9,10},{10,1... | collective-permute-start | bytes 393224 | tf_op jit(solution)/shard_map/ppermute | solution.py:323

commit v4 on v3

--- a/solution.py
+++ b/solution.py
@@ -6,7 +6,8 @@
 from jax.sharding import PartitionSpec as P
 
 HR = 2
-GROUPS = ((2,), (3,), (1,), (0,))
+GROUPS = ((2,), (3, 1), (0,))
+BACK = (2, 1, 3)
 STAGES = (2, 6)
 LATER = 0
 K1_LIMIT = 24
@@ -330,7 +331,10 @@
     parts = lax.all_to_all(total.reshape(zs, levels // zs, width // xs), "z", 0, 0)
     column = lax.all_to_all(sum_received(parts, factor), "z", 0, 0)
     column = column.reshape(levels, width // xs)
-    return assemble([column] + [along_x(column, k) for k in range(1, xs)])
+    others = {}
+    for k in BACK:
+        others[k] = along_x(column, k)
+    return assemble([column] + [others[k] for k in range(1, xs)])
 
 
 def solution(mesh):

time: 65.6 us -> 65.4 us (level)
    pallas_call x4 -> x3, Pallas kernels: 5.81 us -> 5.61 us  [member_sums(): pl.pallas_call(kernel, out_shape=pieces if halo is None else (smoothed,)...]
where the time goes in v4:
time: 65.4 us; the launch traced here: 65.3 us
  blocking collectives  28.9 us (44%)
  Pallas kernels  13.8 us (21%)
  waiting for transfers between devices  13.1 us (20%)
  starting transfers between devices  9.28 us (14%)
    all_to_all x1, blocking collectives, increment(): lax.all_to_all(total.reshape(zs, levels // zs, width // xs), 'z', 0, 0)  17.5 us
    ppermute x6, waiting for transfers between devices, along_x(): return lax.ppermute(piece, 'x', [(i, (i + k) % xs) for i in range(xs)])  12.7 us
    all_to_all x1, blocking collectives, increment(): column = lax.all_to_all(sum_received(parts, factor), 'z', 0, 0)  11.5 us
    ppermute x6, starting transfers between devices, along_x(): return lax.ppermute(piece, 'x', [(i, (i + k) % xs) for i in range(xs)])  7.15 us
    pallas_call x1, Pallas kernels, smooth_own(): pl.pallas_call(kernel, out_shape=(jax.ShapeDtypeStruct((blocks, rows, bre...  6.02 us
    pallas_call x3, Pallas kernels, member_sums(): pl.pallas_call(kernel, out_shape=pieces if halo is None else (smoothed,)...  5.61 us
    ppermute x1, starting transfers between devices, tile_halos(): lax.ppermute(second, 'dom', within)  1.86 us
  transfers between devices with their start and end apart: 8, of which 6 were waited for; matrix products, arithmetic and copies ran while one was open for 0% of the time, Pallas kernels for 11%

profile of v4, /device:TPU:24, one launch (start us, length us, event | category | flops | bytes accessed | tf_op | source)
XLA Modules:
  0.0 65.3 jit_solution(2694810742147486536)
XLA Ops:
  0.0 0.0 copy-start
  0.0 1.2 %tile_edges.1 = (bf16[1024,256]{1,0:T(8,128)(2,1)S(1)}, bf16[1024,256]{1,0:T(8,128)(2,1)S(1)}) custom-call(bf16[1024,2048]{1,0:T(8,128)(2,1)} %bitcast.10), custom_call_target="tpu_custom_call" | custom-call | tf_op jit(solution)/shard_map/tile_edges/pallas_call | solution.py:40
  1.2 0.3 collective-permute-start
  1.5 1.9 %collective-permute-start.1 = (bf16[1024,256]{1,0:T(8,128)(2,1)S(1)}, bf16[1024,256]{1,0:T(8,128)(2,1)S(1)}, u32[]{:S(2)}, u32[]{:S(2)}) collective-permute-start(bf16[1024,256]{1,0:T(8,128)(2,1)S(1)} %get-tuple-element.22), channel_id=1, source_target_pairs={{0,32},{32,0},{64,96},{96,64},{128,160},{160,128},{192,224},{224,1... | collective-permute-start | bytes 1572872 | tf_op jit(solution)/shard_map/ppermute | solution.py:52
  3.4 0.0 copy-done
  3.4 0.1 copy.9.index
  3.5 6.0 %smooth_own.1 = (bf16[16,1024,128]{2,1,0:T(8,128)(2,1)S(1)}, f32[2,1024,256]{2,1,0:T(8,128)S(1)}, bf16[2,256,256]{2,1,0:T(8,128)(2,1)S(1)}, bf16[16,4,128,128]{3,2,1,0:T(8,128)(2,1)S(1)}, bf16[1024,2048]{1,0:T(8,128)(2,1)S(1)}) custom-call(s32[4,16]{1,0:T(4,128)} %bitcast.13, bf16[1024,2048]{1,0:T(8,128)(2,1)} %bitcast.11, ...), custom_call_target="tpu_custom_call" | custom-call | flops 2147483648 | bytes 8388608 | tf_op jit(solution)/shard_map/smooth_own/pallas_call | solution.py:153
  9.5 0.4 collective-permute-done.refs_3_
  9.9 0.0 collective-permute-done.1.refs_4_
  9.9 1.7 %member_sums.3 = (bf16[16,1024,128]{2,1,0:T(8,128)(2,1)S(1)}, bf16[128,512]{1,0:T(8,128)(2,1)S(1)}) custom-call(s32[16,4]{1,0:T(8,128)S(1)} %copy.9.index, bf16[16,4,128,128]{3,2,1,0:T(8,128)(2,1)S(1)} %get-tuple-element.16.interp, bf16[1024,2048]{1,0:T(8,128)(2,1)S(1)} %get-tuple-element.17.pert, ...), custom_call_target="tpu_custom_call", output_to_operand_aliasing={{0}: (3, {})} | custom-call | flops 671088640 | bytes 3145728 | tf_op jit(solution)/shard_map/member_sums/pallas_call | solution.py:228
  11.6 2.6 %member_sums.5 = (bf16[128,512]{1,0:T(8,128)(2,1)S(1)}, bf16[128,512]{1,0:T(8,128)(2,1)S(1)}) custom-call(s32[16,4]{1,0:T(8,128)S(1)} %copy.9.index, bf16[16,4,128,128]{3,2,1,0:T(8,128)(2,1)S(1)} %get-tuple-element.16.interp, bf16[1024,2048]{1,0:T(8,128)(2,1)S(1)} %get-tuple-element.17.pert, bf16[16,1024,128]{2,1,0:T(8,128)(2,1)S(1)} %get-tuple-element.23.refs_0_), custom_call_target="tpu_custom_call" | custom-call | flops 1207959552 | bytes 6291456 | tf_op jit(solution)/shard_map/member_sums/pallas_call | solution.py:228
  14.2 2.8 %collective-permute-start.3 = (bf16[128,512]{1,0:T(8,128)(2,1)S(1)}, bf16[128,512]{1,0:T(8,128)(2,1)S(1)}, u32[]{:S(2)}, u32[]{:S(2)}) collective-permute-start(bf16[128,512]{1,0:T(8,128)(2,1)S(1)} %get-tuple-element.25), channel_id=1, source_target_pairs={{0,3},{1,0},{2,1},{3,2},{4,7},{5,4},{6,5},{7,6},{8,11},{9,8},{10,9... | collective-permute-start | bytes 393224 | tf_op jit(solution)/shard_map/ppermute | solution.py:324
  17.0 0.0 collective-permute-start.4
  17.0 2.3 %collective-permute-start.2 = (bf16[128,512]{1,0:T(8,128)(2,1)S(1)}, bf16[128,512]{1,0:T(8,128)(2,1)S(1)}, u32[]{:S(2)}, u32[]{:S(2)}) collective-permute-start(bf16[128,512]{1,0:T(8,128)(2,1)S(1)} %get-tuple-element.24), channel_id=1, source_target_pairs={{0,2},{1,3},{2,0},{3,1},{4,6},{5,7},{6,4},{7,5},{8,10},{9,11},{10,... | collective-permute-start | bytes 393224 | tf_op jit(solution)/shard_map/ppermute | solution.py:324
  19.3 1.4 %member_sums.4.refs_0_ = bf16[128,512]{1,0:T(8,128)(2,1)S(1)} custom-call(s32[16,4]{1,0:T(8,128)S(1)} %copy.9.index, bf16[16,4,128,128]{3,2,1,0:T(8,128)(2,1)S(1)} %get-tuple-element.16.interp, bf16[1024,2048]{1,0:T(8,128)(2,1)S(1)} %get-tuple-element.17.pert, bf16[16,1024,128]{2,1,0:T(8,128)(2,1)S(1)} %get-tuple-element.23.refs_0_), custom_call_target="tpu_custom_call" | custom-call | flops 671088640 | bytes 3145728 | tf_op jit(solution)/shard_map/member_sums/pallas_call | solution.py:228
  20.7 0.2 collective-permute-done.3.refs_2_
  20.9 6.3 %collective-permute-done.4.refs_3_ = bf16[128,512]{1,0:T(8,128)(2,1)S(1)} collective-permute-done((bf16[128,512]{1,0:T(8,128)(2,1)S(1)}, bf16[128,512]{1,0:T(8,128)(2,1)S(1)}, u32[]{:S(2)}, u32[]{:S(2)}) %collective-permute-start.4) | collective-permute-done | bytes 131104 | tf_op jit(solution)/shard_map/ppermute | solution.py:324
  27.2 0.0 collective-permute-done.2.refs_1_
  27.2 0.1 sum_pieces.1
  27.3 17.5 %all_to_all.10.parts_ref = bf16[8,16,512]{2,1,0:T(8,128)(2,1)S(1)} all-to-all(bf16[8,16,512]{2,1,0:T(8,128)(2,1)S(1)} %bitcast.5), channel_id=1, replica_groups=mesh['dom'=8,'z'=8,'x'=4] {'z'}, dimensions={0} | all-to-all | bytes 262144 | tf_op jit(solution)/shard_map/all_to_all | solution.py:331
  44.8 11.5 %all_to_all.11 = bf16[8,16,512]{2,1,0:T(8,128)(2,1)S(1)} all-to-all(bf16[8,16,512]{2,1,0:T(8,128)(2,1)S(1)} %sum_received.1), channel_id=1, replica_groups=mesh['dom'=8,'z'=8,'x'=4] {'z'}, dimensions={0} | all-to-all | bytes 262144 | tf_op jit(solution)/shard_map/all_to_all | solution.py:332
  56.2 0.3 collective-permute-start.7
  56.6 0.5 collective-permute-start.6
  57.0 1.2 %collective-permute-start.5 = (bf16[128,512]{1,0:T(8,128)(2,1)S(1)}, bf16[128,512]{1,0:T(8,128)(2,1)S(1)}, u32[]{:S(2)}, u32[]{:S(2)}) collective-permute-start(bf16[128,512]{1,0:T(8,128)(2,1)S(1)} %bitcast.8), channel_id=1, source_target_pairs={{0,1},{1,2},{2,3},{3,0},{4,5},{5,6},{6,7},{7,4},{8,9},{9,10},{10,1... | collective-permute-start | bytes 393224 | tf_op jit(solution)/shard_map/ppermute | solution.py:324
  58.3 2.9 %collective-permute-done.7.refs_3_ = bf16[128,512]{1,0:T(8,128)(2,1)S(1)} collective-permute-done((bf16[128,512]{1,0:T(8,128)(2,1)S(1)}, bf16[128,512]{1,0:T(8,128)(2,1)S(1)}, u32[]{:S(2)}, u32[]{:S(2)}) %collective-permute-start.7) | collective-permute-done | bytes 131104 | tf_op jit(solution)/shard_map/ppermute | solution.py:324
  61.2 1.9 %collective-permute-done.6.refs_2_ = bf16[128,512]{1,0:T(8,128)(2,1)S(1)} collective-permute-done((bf16[128,512]{1,0:T(8,128)(2,1)S(1)}, bf16[128,512]{1,0:T(8,128)(2,1)S(1)}, u32[]{:S(2)}, u32[]{:S(2)}) %collective-permute-start.6) | collective-permute-done | bytes 131104 | tf_op jit(solution)/shard_map/ppermute | solution.py:324
  63.1 1.3 %collective-permute-done.5.refs_1_ = bf16[128,512]{1,0:T(8,128)(2,1)S(1)} collective-permute-done((bf16[128,512]{1,0:T(8,128)(2,1)S(1)}, bf16[128,512]{1,0:T(8,128)(2,1)S(1)}, u32[]{:S(2)}, u32[]{:S(2)}) %collective-permute-start.5) | collective-permute-done | bytes 131104 | tf_op jit(solution)/shard_map/ppermute | solution.py:324
  64.4 0.8 %assemble.1 = bf16[128,2048]{1,0:T(8,128)(2,1)} custom-call(bf16[128,512]{1,0:T(8,128)(2,1)S(1)} %bitcast.9, bf16[128,512]{1,0:T(8,128)(2,1)S(1)} %collective-permute-done.5.refs_1_, bf16[128,512]{1,0:T(8,128)(2,1)S(1)} %collective-permute-done.6.refs_2_, bf16[128,512]{1,0:T(8,128)(2,1)S(1)} %collective-permute-done.7.refs_3_), custom_call_target="tpu_custom_call" | custom-call | tf_op jit(solution)/shard_map/assemble/pallas_call | solution.py:291
  (1 shorter events, 0.0 us)
Async XLA Ops:
  0.0 3.4 %copy-start = (s32[16,4]{0,1:T(4,128)S(1)}, s32[16,4]{0,1:T(4,128)}, u32[]{:S(2)}) copy-start(s32[16,4]{0,1:T(4,128)} %param.9) | copy-start | bytes 772
  1.2 8.7 %collective-permute-start = (bf16[1024,256]{1,0:T(8,128)(2,1)S(1)}, bf16[1024,256]{1,0:T(8,128)(2,1)S(1)}, u32[]{:S(2)}, u32[]{:S(2)}) collective-permute-start(bf16[1024,256]{1,0:T(8,128)(2,1)S(1)} %get-tuple-element.21), channel_id=1, source_target_pairs={{0,224},{32,64},{64,32},{96,128},{128,96},{160,192},{192,160},{224... | collective-permute-start | bytes 1572872 | tf_op jit(solution)/shard_map/ppermute | solution.py:52
  1.5 8.4 %collective-permute-start.1 = (bf16[1024,256]{1,0:T(8,128)(2,1)S(1)}, bf16[1024,256]{1,0:T(8,128)(2,1)S(1)}, u32[]{:S(2)}, u32[]{:S(2)}) collective-permute-start(bf16[1024,256]{1,0:T(8,128)(2,1)S(1)} %get-tuple-element.22), channel_id=1, source_target_pairs={{0,32},{32,0},{64,96},{96,64},{128,160},{160,128},{192,224},{224,1... | collective-permute-start | bytes 1572872 | tf_op jit(solution)/shard_map/ppermute | solution.py:52
  14.2 6.7 %collective-permute-start.3 = (bf16[128,512]{1,0:T(8,128)(2,1)S(1)}, bf16[128,512]{1,0:T(8,128)(2,1)S(1)}, u32[]{:S(2)}, u32[]{:S(2)}) collective-permute-start(bf16[128,512]{1,0:T(8,128)(2,1)S(1)} %get-tuple-element.25), channel_id=1, source_target_pairs={{0,3},{1,0},{2,1},{3,2},{4,7},{5,4},{6,5},{7,6},{8,11},{9,8},{10,9... | collective-permute-start | bytes 393224 | tf_op jit(solution)/shard_map/ppermute | solution.py:324
  17.0 10.2 %collective-permute-start.4 = (bf16[128,512]{1,0:T(8,128)(2,1)S(1)}, bf16[128,512]{1,0:T(8,128)(2,1)S(1)}, u32[]{:S(2)}, u32[]{:S(2)}) collective-permute-start(bf16[128,512]{1,0:T(8,128)(2,1)S(1)} %get-tuple-element.26), channel_id=1, source_target_pairs={{0,1},{1,2},{2,3},{3,0},{4,5},{5,6},{6,7},{7,4},{8,9},{9,10},{10,1... | collective-permute-start | bytes 393224 | tf_op jit(solution)/shard_map/ppermute | solution.py:324
  17.0 10.2 %collective-permute-start.2 = (bf16[128,512]{1,0:T(8,128)(2,1)S(1)}, bf16[128,512]{1,0:T(8,128)(2,1)S(1)}, u32[]{:S(2)}, u32[]{:S(2)}) collective-permute-start(bf16[128,512]{1,0:T(8,128)(2,1)S(1)} %get-tuple-element.24), channel_id=1, source_target_pairs={{0,2},{1,3},{2,0},{3,1},{4,6},{5,7},{6,4},{7,5},{8,10},{9,11},{10,... | collective-permute-start | bytes 393224 | tf_op jit(solution)/shard_map/ppermute | solution.py:324
  56.2 5.0 %collective-permute-start.7 = (bf16[128,512]{1,0:T(8,128)(2,1)S(1)}, bf16[128,512]{1,0:T(8,128)(2,1)S(1)}, u32[]{:S(2)}, u32[]{:S(2)}) collective-permute-start(bf16[128,512]{1,0:T(8,128)(2,1)S(1)} %bitcast.6), channel_id=1, source_target_pairs={{0,3},{1,0},{2,1},{3,2},{4,7},{5,4},{6,5},{7,6},{8,11},{9,8},{10,9... | collective-permute-start | bytes 393224 | tf_op jit(solution)/shard_map/ppermute | solution.py:324
  56.6 6.5 %collective-permute-start.6 = (bf16[128,512]{1,0:T(8,128)(2,1)S(1)}, bf16[128,512]{1,0:T(8,128)(2,1)S(1)}, u32[]{:S(2)}, u32[]{:S(2)}) collective-permute-start(bf16[128,512]{1,0:T(8,128)(2,1)S(1)} %bitcast.7), channel_id=1, source_target_pairs={{0,2},{1,3},{2,0},{3,1},{4,6},{5,7},{6,4},{7,5},{8,10},{9,11},{10,... | collective-permute-start | bytes 393224 | tf_op jit(solution)/shard_map/ppermute | solution.py:324
  57.0 7.4 %collective-permute-start.5 = (bf16[128,512]{1,0:T(8,128)(2,1)S(1)}, bf16[128,512]{1,0:T(8,128)(2,1)S(1)}, u32[]{:S(2)}, u32[]{:S(2)}) collective-permute-start(bf16[128,512]{1,0:T(8,128)(2,1)S(1)} %bitcast.8), channel_id=1, source_target_pairs={{0,1},{1,2},{2,3},{3,0},{4,5},{5,6},{6,7},{7,4},{8,9},{9,10},{10,1... | collective-permute-start | bytes 393224 | tf_op jit(solution)/shard_map/ppermute | solution.py:324
